TPU v7x, 32 devices: a whole 2x2x4 slice. The times are simulated.
32 devices in a mesh: lat: 8 (over y, x, core), lev: 4 (over z).
Axes of the slice: x: 2, y: 2, z: 4, core: 2. Of those that a mesh axis runs over, the one named last changes fastest.
Arguments:
- fields: float32 [12, 128, 256, 1024], P(None, 'lev', 'lat'), may hold values from -6 to 6
- legendre: bfloat16 [256, 256, 256], P('lat'), as said below
- owner_counts: int32 [8], replicated, may hold values from 1 to 64, 256 in all
Outputs:
- covariance: float32 [512, 128, 128], P('lat', 'lev')
Inputs may be any that keep to these rules, and one draw needn't show every extreme that they name: `owner_counts`: each owner holds 1 to 64 total wavenumbers, the counts sum to 256, and some owner holds exactly 64. legendre[lat, m, n] is zero where n < m.
All inputs are finite; a program needn't handle non-finite values.
Results may differ from a plain program's by a relative error of at most 0.0038.
Values may be sent and summed in bfloat16 or wider, within the bound.
A program may use at most 192 MiB of HBM per device.

v0:
```python
import functools
import math

import jax
import jax.numpy as jnp
import numpy as np
from jax import lax
from jax.experimental import pallas as pl
from jax.experimental.pallas import tpu as pltpu
from jax.sharding import PartitionSpec as P


def fourier_table(points, modes):
    places = jnp.arange(points, dtype=jnp.int32)
    orders = jnp.arange(modes, dtype=jnp.int32)
    phase = places[:, None] * orders[None, :] % points
    angle = phase.astype(jnp.float32) * (2.0 * math.pi / points)
    factor = points ** (-0.5)
    return jnp.stack([jnp.cos(angle) * factor, -jnp.sin(angle) * factor], axis=2)


def plain_on_device(fields, legendre, owner_counts):
    members, lev_rows, lat_rows, points = fields.shape
    modes = legendre.shape[1]
    lev_count = lax.axis_size("lev")
    owners = owner_counts.shape[0]
    capacity = 2 * modes // owners
    dft_table = fourier_table(points, modes)
    spectra = jnp.einsum("belx,xmc->lmcbe", fields, dft_table, precision=lax.Precision.HIGHEST)
    spectra = spectra.reshape(lat_rows, modes, 2 * members * lev_rows).astype(jnp.bfloat16)
    collected_rows, transform_table_rows = (
        lax.all_to_all(spectra, "lat", split_axis=1, concat_axis=0, tiled=True),
        lax.all_to_all(legendre, "lat", split_axis=1, concat_axis=0, tiled=True),
    )
    wavenumber_rows = jnp.einsum(
        "dez,det->tez", collected_rows, transform_table_rows, preferred_element_type=jnp.float32
    )
    resident_modes = wavenumber_rows.shape[1]
    shaped = wavenumber_rows.reshape(modes, resident_modes, 2, members, lev_rows)
    anomaly = (shaped - jnp.mean(shaped, axis=3, keepdims=True)).astype(jnp.bfloat16)
    anomaly = anomaly.reshape(modes, resident_modes, 2 * members * lev_rows)
    starts = jnp.cumsum(owner_counts) - owner_counts
    offset = jnp.arange(capacity, dtype=jnp.int32)
    active_flag = offset[None, :] < owner_counts[:, None]
    slot_index = jnp.where(active_flag, starts[:, None] + offset[None, :], 0).reshape(-1)
    slotted = jnp.take(anomaly, slot_index, axis=0)
    slotted = jnp.where(active_flag.reshape(-1)[:, None, None], slotted, jnp.zeros_like(slotted))
    slotted = slotted[None]
    received = lax.all_to_all(
        lax.all_to_all(slotted, "lat", split_axis=1, concat_axis=2, tiled=True),
        "lev",
        split_axis=2,
        concat_axis=0,
        tiled=True,
    )
    mode_share = received.shape[2]
    blocks = received.reshape(lev_count, capacity, mode_share, 2 * members, lev_rows)
    partial_value = jnp.einsum(
        "esaql,fsaqk->selfk", blocks, blocks, preferred_element_type=jnp.float32
    )
    partial_value = partial_value.reshape(capacity, lev_count * lev_rows, lev_count * lev_rows)
    summed = lax.psum_scatter(partial_value, "lev", scatter_dimension=1, tiled=True)
    owner = lax.axis_index("lat")
    wavenumber = starts[owner] + offset
    live_count = owner_counts[owner]
    divisor = ((members - 1) * (2 * wavenumber + 2)).astype(jnp.float32)
    scaled = summed / divisor[:, None, None]
    return jnp.where((offset < live_count)[:, None, None], scaled, jnp.zeros_like(scaled))


LANES = 128
VMEM_LIMIT = 60 * 1024 * 1024


def split_bf16(values):
    high = values.astype(jnp.bfloat16)
    return high, (values - high.astype(jnp.float32)).astype(jnp.bfloat16)


def folded_tables(points, orders):
    tables = []
    for residues, length in (((1, 3), points // 2), ((0,), points // 4), ((2,), points // 4)):
        m = orders[np.isin(orders % 4, residues)]
        angle = 2.0 * np.pi * ((m[:, None] * np.arange(length)[None, :]) % points) / points
        table = np.concatenate([np.cos(angle), -np.sin(angle)]) * points ** -0.5
        table = table.astype(np.float32)
        high = table.astype(jnp.bfloat16)
        low = (table - high.astype(np.float32)).astype(jnp.bfloat16)
        tables.append(np.stack([high, low]))
    return tables


NT = (((1,), (1,)), ((), ()))
TN = (((0,), (0,)), ((), ()))


def dft_kernel(runs, width, pieces, *refs):
    field_refs = refs[:pieces]
    odd_ref, zero_ref, two_ref, out_ref, held = refs[pieces:]
    rows, lats, _ = field_refs[0].shape
    quarter = pieces * LANES // 4
    lines = [ref.reshape(rows * lats, LANES) for ref in field_refs]

    def fetch(lat):
        return [
            jnp.concatenate([line[pl.ds(lat + s, rows, lats), :] for s in range(2)], axis=0)
            for line in lines
        ]

    def transform(table_ref, values):
        high, low = split_bf16(values)
        dot = functools.partial(lax.dot_general, dimension_numbers=NT, preferred_element_type=jnp.float32)
        return dot(table_ref[0], high) + (dot(table_ref[1], high) + dot(table_ref[0], low))

    def put(lat, lane, kind, sums):
        count = sums.shape[0] // 2
        for q in range(2):
            done = 0
            for start in runs[kind]:
                held[q, pl.ds(start * lats + lat, width, lats), :] = (
                    sums[q * count + done:q * count + done + width, lane:lane + LANES]
                )
                done += width

    def step(pair, carry):
        lat = 2 * pair
        values = fetch(lat)
        middle = len(values) // 2
        even = jnp.concatenate([u + v for u, v in zip(values[:middle], values[middle:])], axis=1)
        odd = jnp.concatenate([u - v for u, v in zip(values[:middle], values[middle:])], axis=1)
        parts = (
            transform(odd_ref, odd),
            transform(zero_ref, even[:, :quarter] + even[:, quarter:]),
            transform(two_ref, even[:, :quarter] - even[:, quarter:]),
        )
        for s in range(2):
            for kind, sums in enumerate(parts):
                put(lat + s, s * LANES, kind, sums)
        return carry

    lax.fori_loop(0, lats // 2, step, 0)
    modes = out_ref.shape[0]
    piece = 32

    def emit(index, carry):
        base = pl.multiple_of(index * piece, piece)
        for q in range(2):
            block = held[q, pl.ds(pl.multiple_of(base * lats, piece * lats), piece * lats), :]
            block = block.astype(jnp.bfloat16).reshape(piece, lats, LANES)
            out_ref[pl.ds(base, piece), :, q * LANES:(q + 1) * LANES] = block
        return carry

    lax.fori_loop(0, modes // piece, emit, 0)


def dft(fields, lat_count, orders, modes):
    members, lev_rows, lat_rows, points = fields.shape
    rows = members * lev_rows
    lats = 16
    width = modes // lat_count
    kinds = [[i for i in range(lat_count) if i % 4 in r] for r in ((1, 3), (0,), (2,))]
    runs = [[i * width for i in kind] for kind in kinds]
    tables = [jnp.asarray(t) for t in folded_tables(points, orders)]
    groups = rows // LANES
    pieces = points // LANES
    return pl.pallas_call(
        functools.partial(dft_kernel, runs, width, pieces),
        grid=(lat_rows // lats, groups),
        out_shape=jax.ShapeDtypeStruct((modes, lat_rows, 2 * rows), jnp.bfloat16),
        in_specs=[
            pl.BlockSpec((LANES, lats, LANES), functools.partial(lambda c, l, g: (g, l, c), c))
            for c in range(pieces)
        ]
        + [pl.BlockSpec(t.shape, lambda l, g: (0, 0, 0)) for t in tables],
        out_specs=pl.BlockSpec((modes, lats, 2 * LANES), lambda l, g: (0, l, g)),
        scratch_shapes=[pltpu.VMEM((2, modes * lats, LANES), jnp.float32)],
        compiler_params=pltpu.CompilerParams(vmem_limit_bytes=VMEM_LIMIT),
        cost_estimate=pl.CostEstimate(flops=15_000_000_000, bytes_accessed=65_000_000, transcendentals=0),
    )(*[fields.reshape(rows, lat_rows, points)] * pieces, *tables)


def legendre_kernel(members, lev_rows, band, x_ref, l_ref, out_ref):
    sources, _, slots, lat_rows, lanes = x_ref.shape
    total = l_ref.shape[-1]
    groups = lanes // (2 * LANES)
    for a in range(slots):
        x = x_ref[:, 0, a].reshape(sources * lat_rows, lanes)
        table = l_ref[:, 0, a, :, band * a:]
        table = table.reshape(sources * lat_rows, total - band * a)
        waves = lax.dot_general(table, x, TN, preferred_element_type=jnp.float32)
        for t in range(a, slots):
            block = waves[(t - a) * band:(t - a + 1) * band]
            row = band * (t * (t + 1) // 2 + a)
            for q in range(2):
                parts = [block[:, (2 * g + q) * LANES:(2 * g + q + 1) * LANES] for g in range(groups)]
                total_sum = functools.reduce(jnp.add, parts)
                shift = LANES // 2
                while shift >= lev_rows:
                    total_sum = total_sum + pltpu.roll(total_sum, shift, 1)
                    shift //= 2
                mean = total_sum * (1.0 / members)
                for g in range(groups):
                    out_ref[0, row:row + band, (2 * g + q) * LANES:(2 * g + q + 1) * LANES] = (
                        parts[g] - mean
                    ).astype(jnp.bfloat16)


def covariance_kernel(band, slots, lev_rows, x_ref, out_ref, held):
    sources, _, lanes = x_ref.shape
    pack = LANES // lev_rows
    groups = lanes // LANES
    per_slot = groups * pack
    for t in range(slots):
        start = band * (t * (t + 1) // 2)

        def spread(a, carry):
            row = pl.multiple_of(start + a * band, band)
            for g in range(groups):
                parts = [
                    x_ref[v, pl.ds(row, band), g * LANES:(g + 1) * LANES].astype(jnp.float32)
                    for v in range(sources)
                ]
                for s in range(pack):
                    joined = jnp.concatenate(
                        [p[:, s * lev_rows:(s + 1) * lev_rows] for p in parts], axis=1
                    )
                    place = (a * per_slot + g * pack + s) * band
                    held[pl.ds(pl.multiple_of(place, band), band), :] = joined
            return carry

        lax.fori_loop(0, t + 1, spread, 0)
        depth = (t + 1) * per_slot

        def multiply(n, carry):
            for s in range(4):
                each = n * 4 + s
                values = held[pl.ds(each, depth, band), :].astype(jnp.bfloat16)
                product = lax.dot_general(values, values, TN, preferred_element_type=jnp.float32)
                out_ref[t * band + each] = product.astype(jnp.bfloat16)
            return carry

        lax.fori_loop(0, band // 4, multiply, 0)


def exchange(values, axis):
    return lax.all_to_all(values, axis, split_axis=0, concat_axis=0, tiled=True)


def on_device(lat_count, lev_count, fields, legendre, owner_counts):
    members, lev_rows, lat_rows, points = fields.shape
    modes, totals = legendre.shape[1:]
    owners = owner_counts.shape[0]
    capacity = 2 * modes // owners
    levels = lev_count * lev_rows
    band = lat_count * lev_count
    slots = modes // band
    lanes = 2 * members * lev_rows
    orders = np.arange(modes).reshape(slots, lev_count, lat_count).transpose(2, 1, 0).reshape(-1)

    table = legendre.reshape(lat_rows, slots, lev_count, lat_count, totals).transpose(3, 2, 1, 0, 4)
    table = exchange(table, "lat")
    spectra = dft(fields, lat_count, orders, modes)
    spectra = exchange(spectra.reshape(lat_count, lev_count, slots, lat_rows, lanes), "lat")

    rows = band * slots * (slots + 1) // 2
    anomaly = pl.pallas_call(
        functools.partial(legendre_kernel, members, lev_rows, band),
        grid=(lev_count,),
        out_shape=jax.ShapeDtypeStruct((lev_count, rows, lanes), jnp.bfloat16),
        in_specs=[
            pl.BlockSpec((lat_count, 1, slots, lat_rows, lanes), lambda j: (0, j, 0, 0, 0)),
            pl.BlockSpec((lat_count, 1, slots, lat_rows, totals), lambda j: (0, j, 0, 0, 0)),
        ],
        out_specs=pl.BlockSpec((1, rows, lanes), lambda j: (j, 0, 0)),
        compiler_params=pltpu.CompilerParams(vmem_limit_bytes=VMEM_LIMIT),
        cost_estimate=pl.CostEstimate(flops=4_000_000_000, bytes_accessed=24_000_000, transcendentals=0),
    )(spectra, table)
    anomaly = exchange(anomaly, "lev")

    partial_value = pl.pallas_call(
        functools.partial(covariance_kernel, band, slots, lev_rows),
        out_shape=jax.ShapeDtypeStruct((totals, levels, levels), jnp.bfloat16),
        in_specs=[pl.BlockSpec(memory_space=pltpu.VMEM)],
        out_specs=pl.BlockSpec(memory_space=pltpu.VMEM),
        scratch_shapes=[pltpu.VMEM((slots * 2 * members * band, levels), jnp.float32)],
        compiler_params=pltpu.CompilerParams(vmem_limit_bytes=VMEM_LIMIT),
        cost_estimate=pl.CostEstimate(flops=2_000_000_000, bytes_accessed=16_000_000, transcendentals=0),
    )(anomaly)

    share = totals // lat_count
    partial_value = exchange(partial_value.reshape(lat_count, share, levels, levels), "lat")
    summed = jnp.sum(partial_value.astype(jnp.float32), axis=0)
    summed = summed.reshape(share, lev_count, lev_rows, levels).transpose(1, 0, 2, 3)
    summed = exchange(summed.astype(jnp.bfloat16), "lev")
    full = jnp.sum(summed.astype(jnp.float32), axis=0)
    full = jnp.broadcast_to(full.astype(jnp.bfloat16)[None], (lat_count, share, lev_rows, levels))
    full = exchange(full, "lat").reshape(totals, lev_rows, levels)

    starts = jnp.cumsum(owner_counts) - owner_counts
    owner = lax.axis_index("lat")
    offset = jnp.arange(capacity, dtype=jnp.int32)
    wavenumber = starts[owner] + offset
    live = offset < owner_counts[owner]
    chosen = jnp.take(full, jnp.where(live, wavenumber, 0), axis=0).astype(jnp.float32)
    divisor = ((members - 1) * (2 * wavenumber + 2)).astype(jnp.float32)
    return jnp.where(live[:, None, None], chosen / divisor[:, None, None], jnp.zeros_like(chosen))


def pick(lat_count, lev_count, fields, legendre, owner_counts):
    members, lev_rows, lat_rows, points = fields.shape
    modes = legendre.shape[1]
    fits = (
        lat_rows % 16 == 0
        and members * lev_rows % LANES == 0
        and lev_rows * lev_count == LANES
        and lat_count % 4 == 0
        and modes % (lat_count * lev_count) == 0
    )
    if fits:
        return on_device(lat_count, lev_count, fields, legendre, owner_counts)
    return plain_on_device(fields, legendre, owner_counts)


def solution(mesh):
    return jax.shard_map(
        functools.partial(pick, mesh.shape["lat"], mesh.shape["lev"]),
        mesh=mesh,
        in_specs=(P(None, "lev", "lat", None), P("lat", None, None), P()),
        out_specs=P("lat", "lev", None),
        check_vma=False,
    )
```

profile of v0, /device:TPU:1, one launch (start us, length us, event | category | flops | bytes accessed | tf_op | source)
XLA Modules:
  0.0 599.8 jit_solution(16903719175058027787)
XLA Ops:
  0.0 6.5 %copy.12 = bf16[32,8,4,8,256]{4,0,1,2,3:T(8,128)(2,1)} copy(bf16[32,8,4,8,256]{4,3,2,1,0:T(8,128)(2,1)} %bitcast.30) | data formatting | bytes 8388608 | tf_op jit(solution)/shard_map/reshape | solution.py:260
  6.5 5.2 all-to-all-start.1
  11.7 64.0 %shard_map.64 = bf16[256,32,768]{2,1,0:T(8,128)(2,1)} custom-call(f32[384,32,1024]{2,1,0:T(8,128)} %bitcast.18, f32[384,32,1024]{2,1,0:T(8,128)} %bitcast.19, f32[384,32,1024]{2,1,0:T(8,128)} %bitcast.20, f32[384,32,1024]{2,1,0:T(8,128)} %bitcast.21, f32[384,32,1024]{2,1,0:T(8,128)} %bitcast.22, f32[384,32,1024]{2,1,0:T(8,128)} %bitcast.23, ...), custom_call_target="tpu_custom_call" | custom-call | flops 15000000512 | bytes 65000000 | tf_op jit(solution)/shard_map/pallas_call | solution.py:166
  75.7 0.0 all-to-all-done.1.l_ref
  75.7 144.6 %all_to_all.30.x_ref = bf16[8,4,8,32,768]{4,3,2,1,0:T(8,128)(2,1)} all-to-all(bf16[8,4,8,32,768]{4,3,2,1,0:T(8,128)(2,1)} %bitcast.26), channel_id=1, replica_groups=mesh['lat'=8,'lev'=4] {'lat'}, dimensions={0} | all-to-all | bytes 25165824 | tf_op jit(solution)/shard_map/all_to_all | solution.py:246
  220.3 17.5 %shard_map.65 = bf16[4,1152,768]{2,1,0:T(8,128)(2,1)} custom-call(bf16[8,4,8,32,768]{4,3,2,1,0:T(8,128)(2,1)} %all_to_all.30.x_ref, bf16[8,4,8,32,256]{4,3,2,1,0:T(8,128)(2,1)} %all-to-all-done.1.l_ref), custom_call_target="tpu_custom_call" | custom-call | flops 4000000000 | bytes 24000000 | tf_op jit(solution)/shard_map/pallas_call | solution.py:266
  237.8 161.9 %all_to_all.31.x_ref = bf16[4,1152,768]{2,1,0:T(8,128)(2,1)} all-to-all(bf16[4,1152,768]{2,1,0:T(8,128)(2,1)} %shard_map.65), channel_id=1, replica_groups=mesh['lat'=8,'lev'=4] {'lev'}, dimensions={0} | all-to-all | bytes 14155776 | tf_op jit(solution)/shard_map/all_to_all | solution.py:246
  399.7 34.9 %shard_map.66 = bf16[256,128,128]{2,1,0:T(8,128)(2,1)} custom-call(bf16[4,1152,768]{2,1,0:T(8,128)(2,1)} %all_to_all.31.x_ref), custom_call_target="tpu_custom_call" | custom-call | flops 2000000000 | bytes 16000000 | tf_op jit(solution)/shard_map/pallas_call | solution.py:280
  434.5 100.3 %all_to_all.32 = bf16[8,32,128,128]{3,2,1,0:T(8,128)(2,1)} all-to-all(bf16[8,32,128,128]{3,2,1,0:T(8,128)(2,1)} %bitcast.27), channel_id=1, replica_groups=mesh['lat'=8,'lev'=4] {'lat'}, dimensions={0} | all-to-all | bytes 16777216 | tf_op jit(solution)/shard_map/all_to_all | solution.py:246
  534.9 5.2 reduce_sum.24
  540.1 0.0 copy-start
  540.1 0.1 copy.10
  540.2 27.2 %all_to_all.33 = bf16[4,32,32,128]{3,2,1,0:T(8,128)(2,1)S(1)} all-to-all(bf16[4,32,32,128]{3,2,1,0:T(8,128)(2,1)S(1)} %copy.10), channel_id=1, replica_groups=mesh['lat'=8,'lev'=4] {'lev'}, dimensions={0} | all-to-all | bytes 2097152 | tf_op jit(solution)/shard_map/all_to_all | solution.py:246
  567.3 0.2 reduce_sum.25
  567.6 1.7 broadcast_in_dim.38
  569.3 5.4 all-to-all-start.5
  574.7 0.0 copy-done
  574.7 0.2 reduce-window.9
  574.9 0.6 dynamic_slice.6
  575.5 0.6 dynamic_slice.7
  576.1 0.7 multiply_convert_fusion
  576.8 1.3 fusion
  578.0 1.3 compare_and_fusion
  579.3 18.6 %all-to-all-done.5 = bf16[8,32,32,128]{3,2,1,0:T(8,128)(2,1)S(1)} async-done(((bf16[8,32,32,128]{3,2,1,0:T(8,128)(2,1)}), bf16[8,32,32,128]{3,2,1,0:T(8,128)(2,1)S(1)}, u32[]{:S(2)}, u32[]{:S(2)}) %all-to-all-start.5) | async-done | bytes 2097184 | tf_op jit(solution)/shard_map/all_to_all | solution.py:246
  597.9 0.7 gather_fusion
  598.5 1.2 divide_select_fusion
  (2 shorter events, 0.0 us)
Async XLA Ops:
  6.5 69.2 %all-to-all-start.1 = ((bf16[8,4,8,32,256]{4,3,2,1,0:T(8,128)(2,1)}), bf16[8,4,8,32,256]{4,3,2,1,0:T(8,128)(2,1)}, u32[]{:S(2)}, u32[]{:S(2)}) async-start(bf16[8,4,8,32,256]{4,3,2,1,0:T(8,128)(2,1)} %bitcast.28), calls=%async_computation.1 | async-start | bytes 8388608 | tf_op jit(solution)/shard_map/all_to_all | solution.py:246
  540.1 34.7 %copy-start = (s32[8]{0:T(128)S(1)}, s32[8]{0:T(128)}, u32[]{:S(2)}) copy-start(s32[8]{0:T(128)} %param.8) | copy-start | bytes 100
  569.3 28.6 %all-to-all-start.5 = ((bf16[8,32,32,128]{3,2,1,0:T(8,128)(2,1)}), bf16[8,32,32,128]{3,2,1,0:T(8,128)(2,1)S(1)}, u32[]{:S(2)}, u32[]{:S(2)}) async-start(bf16[8,32,32,128]{3,2,1,0:T(8,128)(2,1)} %broadcast_in_dim.38), calls=%async_computation.5 | async-start | bytes 4194304 | tf_op jit(solution)/shard_map/all_to_all | solution.py:246
where the time goes:
time: 604 us; the launch traced here: 600 us
  blocking collectives  434 us (72%)
  Pallas kernels  116 us (19%)
  waiting for transfers between devices  18.6 us (3%)
  starting transfers between devices  10.7 us (2%)
  local copies, waits for them, and re-layouts  10.1 us (2%)
  other arithmetic  10.1 us (2%)
    all_to_all x4, blocking collectives, exchange(): return lax.all_to_all(values, axis, split_axis=0, concat_axis=0, tiled=True)  434 us
    pallas_call x1, Pallas kernels, dft(): pl.pallas_call(functools.partial(dft_kernel, runs, width, pieces), grid=(...  64 us
    pallas_call x1, Pallas kernels, on_device(): pl.pallas_call(functools.partial(covariance_kernel, band, slots, lev_rows...  34.9 us
    all_to_all x2, waiting for transfers between devices, exchange(): return lax.all_to_all(values, axis, split_axis=0, concat_axis=0, tiled=True)  18.6 us
    pallas_call x1, Pallas kernels, on_device(): pl.pallas_call(functools.partial(legendre_kernel, members, lev_rows, band...  17.5 us
  transfers between devices with their start and end apart: 2, of which 1 were waited for; matrix products, arithmetic and copies ran while one was open for 1% of the time, Pallas kernels for 11%

commit v1 on v0

--- a/solution.py
+++ b/solution.py
@@ -70,6 +70,7 @@
 
 LANES = 128
 VMEM_LIMIT = 60 * 1024 * 1024
+PAIRS = 2
 
 
 def split_bf16(values):
@@ -94,9 +95,10 @@
 TN = (((0,), (0,)), ((), ()))
 
 
-def dft_kernel(runs, width, pieces, *refs):
+def dft_kernel(runs, width, pieces, pairs, *refs):
     field_refs = refs[:pieces]
-    odd_ref, zero_ref, two_ref, out_ref, held = refs[pieces:]
+    odd_ref, zero_ref, two_ref = refs[pieces:pieces + 3]
+    out_refs, held = refs[pieces + 3:-1], refs[-1]
     rows, lats, _ = field_refs[0].shape
     quarter = pieces * LANES // 4
     lines = [ref.reshape(rows * lats, LANES) for ref in field_refs]
@@ -113,14 +115,12 @@
         return dot(table_ref[0], high) + (dot(table_ref[1], high) + dot(table_ref[0], low))
 
     def put(lat, lane, kind, sums):
-        count = sums.shape[0] // 2
-        for q in range(2):
-            done = 0
-            for start in runs[kind]:
-                held[q, pl.ds(start * lats + lat, width, lats), :] = (
-                    sums[q * count + done:q * count + done + width, lane:lane + LANES]
-                )
-                done += width
+        done = 0
+        for start in runs[kind]:
+            held[pl.ds(start * lats + lat, width, lats), :] = (
+                sums[done:done + width, lane:lane + LANES]
+            )
+            done += width
 
     def step(pair, carry):
         lat = 2 * pair
@@ -139,60 +139,68 @@
         return carry
 
     lax.fori_loop(0, lats // 2, step, 0)
-    modes = out_ref.shape[0]
-    piece = 32
+    piece = width // pairs
 
     def emit(index, carry):
-        base = pl.multiple_of(index * piece, piece)
-        for q in range(2):
-            block = held[q, pl.ds(pl.multiple_of(base * lats, piece * lats), piece * lats), :]
+        for c, out_ref in enumerate(out_refs):
+            base = pl.multiple_of(index * width + c * piece, piece)
+            block = held[pl.ds(pl.multiple_of(base * lats, piece * lats), piece * lats), :]
             block = block.astype(jnp.bfloat16).reshape(piece, lats, LANES)
-            out_ref[pl.ds(base, piece), :, q * LANES:(q + 1) * LANES] = block
+            out_ref[pl.ds(pl.multiple_of(index * piece, piece), piece), :, :] = block
         return carry
 
-    lax.fori_loop(0, modes // piece, emit, 0)
-
-
-def dft(fields, lat_count, orders, modes):
+    lax.fori_loop(0, out_refs[0].shape[0] // piece, emit, 0)
+
+
+def dft(fields, lat_count, orders, modes, q, pairs):
     members, lev_rows, lat_rows, points = fields.shape
     rows = members * lev_rows
     lats = 16
     width = modes // lat_count
     kinds = [[i for i in range(lat_count) if i % 4 in r] for r in ((1, 3), (0,), (2,))]
     runs = [[i * width for i in kind] for kind in kinds]
-    tables = [jnp.asarray(t) for t in folded_tables(points, orders)]
+    tables = []
+    for t in folded_tables(points, orders):
+        count = t.shape[1] // 2
+        tables.append(jnp.asarray(t[:, q * count:(q + 1) * count]))
     groups = rows // LANES
     pieces = points // LANES
     return pl.pallas_call(
-        functools.partial(dft_kernel, runs, width, pieces),
+        functools.partial(dft_kernel, runs, width, pieces, pairs),
         grid=(lat_rows // lats, groups),
-        out_shape=jax.ShapeDtypeStruct((modes, lat_rows, 2 * rows), jnp.bfloat16),
+        out_shape=[jax.ShapeDtypeStruct((modes // pairs, lat_rows, rows), jnp.bfloat16)] * pairs,
         in_specs=[
             pl.BlockSpec((LANES, lats, LANES), functools.partial(lambda c, l, g: (g, l, c), c))
             for c in range(pieces)
         ]
         + [pl.BlockSpec(t.shape, lambda l, g: (0, 0, 0)) for t in tables],
-        out_specs=pl.BlockSpec((modes, lats, 2 * LANES), lambda l, g: (0, l, g)),
-        scratch_shapes=[pltpu.VMEM((2, modes * lats, LANES), jnp.float32)],
+        out_specs=[pl.BlockSpec((modes // pairs, lats, LANES), lambda l, g: (0, l, g))] * pairs,
+        scratch_shapes=[pltpu.VMEM((modes * lats, LANES), jnp.float32)],
         compiler_params=pltpu.CompilerParams(vmem_limit_bytes=VMEM_LIMIT),
         cost_estimate=pl.CostEstimate(flops=15_000_000_000, bytes_accessed=65_000_000, transcendentals=0),
     )(*[fields.reshape(rows, lat_rows, points)] * pieces, *tables)
 
 
 def legendre_kernel(members, lev_rows, band, x_ref, l_ref, out_ref):
-    sources, _, slots, lat_rows, lanes = x_ref.shape
+    sources, inner, _, lat_rows, lanes = x_ref.shape
+    targets = out_ref.shape[0]
+    slots = x_ref.shape[2]
     total = l_ref.shape[-1]
-    groups = lanes // (2 * LANES)
+    part = band // targets
+    groups = lanes // LANES
     for a in range(slots):
-        x = x_ref[:, 0, a].reshape(sources * lat_rows, lanes)
-        table = l_ref[:, 0, a, :, band * a:]
-        table = table.reshape(sources * lat_rows, total - band * a)
-        waves = lax.dot_general(table, x, TN, preferred_element_type=jnp.float32)
+        waves = []
+        for i in range(inner):
+            x = x_ref[:, i, a].reshape(sources * lat_rows, lanes)
+            table = l_ref[:, i, a, :, band * a:]
+            table = table.reshape(sources * lat_rows, total - band * a)
+            waves.append(lax.dot_general(table, x, TN, preferred_element_type=jnp.float32))
         for t in range(a, slots):
-            block = waves[(t - a) * band:(t - a + 1) * band]
-            row = band * (t * (t + 1) // 2 + a)
-            for q in range(2):
-                parts = [block[:, (2 * g + q) * LANES:(2 * g + q + 1) * LANES] for g in range(groups)]
+            row = inner * part * (t * (t + 1) // 2 + a)
+            for z in range(targets):
+                at = (t - a) * band + z * part
+                block = jnp.concatenate([w[at:at + part] for w in waves], axis=0)
+                parts = [block[:, g * LANES:(g + 1) * LANES] for g in range(groups)]
                 total_sum = functools.reduce(jnp.add, parts)
                 shift = LANES // 2
                 while shift >= lev_rows:
@@ -200,46 +208,49 @@
                     shift //= 2
                 mean = total_sum * (1.0 / members)
                 for g in range(groups):
-                    out_ref[0, row:row + band, (2 * g + q) * LANES:(2 * g + q + 1) * LANES] = (
+                    out_ref[z, row:row + inner * part, g * LANES:(g + 1) * LANES] = (
                         parts[g] - mean
                     ).astype(jnp.bfloat16)
 
 
-def covariance_kernel(band, slots, lev_rows, x_ref, out_ref, held):
-    sources, _, lanes = x_ref.shape
+def covariance_kernel(part, inner, slots, lev_rows, *refs):
+    x_refs, out_ref, held = refs[:-2], refs[-2], refs[-1]
+    sources, _, lanes = x_refs[0].shape
     pack = LANES // lev_rows
     groups = lanes // LANES
-    per_slot = groups * pack
+    rows = inner * part
+    per_slot = len(x_refs) * groups * pack * rows
     for t in range(slots):
-        start = band * (t * (t + 1) // 2)
+        start = rows * (t * (t + 1) // 2)
 
         def spread(a, carry):
-            row = pl.multiple_of(start + a * band, band)
-            for g in range(groups):
-                parts = [
-                    x_ref[v, pl.ds(row, band), g * LANES:(g + 1) * LANES].astype(jnp.float32)
-                    for v in range(sources)
-                ]
-                for s in range(pack):
-                    joined = jnp.concatenate(
-                        [p[:, s * lev_rows:(s + 1) * lev_rows] for p in parts], axis=1
-                    )
-                    place = (a * per_slot + g * pack + s) * band
-                    held[pl.ds(pl.multiple_of(place, band), band), :] = joined
+            row = pl.multiple_of(start + a * rows, rows)
+            for c, x_ref in enumerate(x_refs):
+                for g in range(groups):
+                    parts = [
+                        x_ref[v, pl.ds(row, rows), g * LANES:(g + 1) * LANES].astype(jnp.float32)
+                        for v in range(sources)
+                    ]
+                    for s in range(pack):
+                        joined = jnp.concatenate(
+                            [p[:, s * lev_rows:(s + 1) * lev_rows] for p in parts], axis=1
+                        )
+                        place = a * per_slot + ((c * groups + g) * pack + s) * rows
+                        held[pl.ds(pl.multiple_of(place, rows), rows), :] = joined
             return carry
 
         lax.fori_loop(0, t + 1, spread, 0)
-        depth = (t + 1) * per_slot
+        depth = (t + 1) * per_slot // part
 
         def multiply(n, carry):
             for s in range(4):
                 each = n * 4 + s
-                values = held[pl.ds(each, depth, band), :].astype(jnp.bfloat16)
+                values = held[pl.ds(each, depth, part), :].astype(jnp.bfloat16)
                 product = lax.dot_general(values, values, TN, preferred_element_type=jnp.float32)
-                out_ref[t * band + each] = product.astype(jnp.bfloat16)
+                out_ref[each, t] = product.astype(jnp.bfloat16)
             return carry
 
-        lax.fori_loop(0, band // 4, multiply, 0)
+        lax.fori_loop(0, part // 4, multiply, 0)
 
 
 def exchange(values, axis):
@@ -253,55 +264,68 @@
     capacity = 2 * modes // owners
     levels = lev_count * lev_rows
     band = lat_count * lev_count
+    part = band // lev_count
     slots = modes // band
-    lanes = 2 * members * lev_rows
+    rows = members * lev_rows
+    pairs = PAIRS
+    inner = lev_count // pairs
     orders = np.arange(modes).reshape(slots, lev_count, lat_count).transpose(2, 1, 0).reshape(-1)
 
     table = legendre.reshape(lat_rows, slots, lev_count, lat_count, totals).transpose(3, 2, 1, 0, 4)
     table = exchange(table, "lat")
-    spectra = dft(fields, lat_count, orders, modes)
-    spectra = exchange(spectra.reshape(lat_count, lev_count, slots, lat_rows, lanes), "lat")
-
-    rows = band * slots * (slots + 1) // 2
-    anomaly = pl.pallas_call(
-        functools.partial(legendre_kernel, members, lev_rows, band),
-        grid=(lev_count,),
-        out_shape=jax.ShapeDtypeStruct((lev_count, rows, lanes), jnp.bfloat16),
-        in_specs=[
-            pl.BlockSpec((lat_count, 1, slots, lat_rows, lanes), lambda j: (0, j, 0, 0, 0)),
-            pl.BlockSpec((lat_count, 1, slots, lat_rows, totals), lambda j: (0, j, 0, 0, 0)),
-        ],
-        out_specs=pl.BlockSpec((1, rows, lanes), lambda j: (j, 0, 0)),
-        compiler_params=pltpu.CompilerParams(vmem_limit_bytes=VMEM_LIMIT),
-        cost_estimate=pl.CostEstimate(flops=4_000_000_000, bytes_accessed=24_000_000, transcendentals=0),
-    )(spectra, table)
-    anomaly = exchange(anomaly, "lev")
+    out_rows = inner * part * slots * (slots + 1) // 2
+    chunks = []
+    for q in range(2):
+        for c, spectra in enumerate(dft(fields, lat_count, orders, modes, q, pairs)):
+            spectra = exchange(spectra.reshape(lat_count, inner, slots, lat_rows, rows), "lat")
+            anomaly = pl.pallas_call(
+                functools.partial(legendre_kernel, members, lev_rows, band),
+                grid=(1,),
+                out_shape=jax.ShapeDtypeStruct((lev_count, out_rows, rows), jnp.bfloat16),
+                in_specs=[
+                    pl.BlockSpec((lat_count, inner, slots, lat_rows, rows), lambda k: (0, 0, 0, 0, 0)),
+                    pl.BlockSpec(
+                        (lat_count, inner, slots, lat_rows, totals),
+                        functools.partial(lambda c, k: (0, c, 0, 0, 0), c),
+                    ),
+                ],
+                out_specs=pl.BlockSpec((lev_count, out_rows, rows), lambda k: (0, 0, 0)),
+                compiler_params=pltpu.CompilerParams(vmem_limit_bytes=VMEM_LIMIT),
+                cost_estimate=pl.CostEstimate(
+                    flops=2_000_000_000, bytes_accessed=12_000_000, transcendentals=0
+                ),
+            )(spectra, table)
+            chunks.append(exchange(anomaly, "lev"))
 
     partial_value = pl.pallas_call(
-        functools.partial(covariance_kernel, band, slots, lev_rows),
-        out_shape=jax.ShapeDtypeStruct((totals, levels, levels), jnp.bfloat16),
-        in_specs=[pl.BlockSpec(memory_space=pltpu.VMEM)],
+        functools.partial(covariance_kernel, part, inner, slots, lev_rows),
+        out_shape=jax.ShapeDtypeStruct((part, slots, levels, levels), jnp.bfloat16),
+        in_specs=[pl.BlockSpec(memory_space=pltpu.VMEM)] * len(chunks),
         out_specs=pl.BlockSpec(memory_space=pltpu.VMEM),
         scratch_shapes=[pltpu.VMEM((slots * 2 * members * band, levels), jnp.float32)],
         compiler_params=pltpu.CompilerParams(vmem_limit_bytes=VMEM_LIMIT),
         cost_estimate=pl.CostEstimate(flops=2_000_000_000, bytes_accessed=16_000_000, transcendentals=0),
-    )(anomaly)
-
-    share = totals // lat_count
-    partial_value = exchange(partial_value.reshape(lat_count, share, levels, levels), "lat")
+    )(*chunks)
+
+    partial_value = exchange(partial_value, "lat")
     summed = jnp.sum(partial_value.astype(jnp.float32), axis=0)
-    summed = summed.reshape(share, lev_count, lev_rows, levels).transpose(1, 0, 2, 3)
-    summed = exchange(summed.astype(jnp.bfloat16), "lev")
-    full = jnp.sum(summed.astype(jnp.float32), axis=0)
-    full = jnp.broadcast_to(full.astype(jnp.bfloat16)[None], (lat_count, share, lev_rows, levels))
-    full = exchange(full, "lat").reshape(totals, lev_rows, levels)
+    summed = summed.reshape(slots, lev_count, lev_rows, levels).transpose(1, 0, 2, 3)
+    full = exchange(summed.astype(jnp.bfloat16), "lev")
+    full = full.transpose(1, 0, 2, 3).reshape(slots * lev_count, lev_rows, levels)
 
     starts = jnp.cumsum(owner_counts) - owner_counts
-    owner = lax.axis_index("lat")
+    share = capacity // lat_count
+    here = lax.axis_index("lat")
+    first = starts // lat_count + (starts % lat_count > here).astype(jnp.int32)
+    rank = first[:, None] + jnp.arange(share, dtype=jnp.int32)[None, :]
+    rank = jnp.minimum(rank, slots * lev_count - 1)
+    sent = jnp.take(full, rank.reshape(-1), axis=0).reshape(owners, share, lev_rows, levels)
+    sent = exchange(sent, "lat").reshape(lat_count * share, lev_rows, levels)
     offset = jnp.arange(capacity, dtype=jnp.int32)
-    wavenumber = starts[owner] + offset
-    live = offset < owner_counts[owner]
-    chosen = jnp.take(full, jnp.where(live, wavenumber, 0), axis=0).astype(jnp.float32)
+    wavenumber = starts[here] + offset
+    place = wavenumber % lat_count * share + offset // lat_count
+    live = offset < owner_counts[here]
+    chosen = jnp.take(sent, place, axis=0).astype(jnp.float32)
     divisor = ((members - 1) * (2 * wavenumber + 2)).astype(jnp.float32)
     return jnp.where(live[:, None, None], chosen / divisor[:, None, None], jnp.zeros_like(chosen))
 
@@ -313,7 +337,10 @@
         lat_rows % 16 == 0
         and members * lev_rows % LANES == 0
         and lev_rows * lev_count == LANES
-        and lat_count % 4 == 0
+        and lat_count % 8 == 0
+        and lev_count % PAIRS == 0
+        and owner_counts.shape[0] == lat_count
+        and 2 * modes // lat_count % lat_count == 0
         and modes % (lat_count * lev_count) == 0
     )
     if fits:

time: 604 us -> 562 us (0.930)
  blocking collectives: 434 us -> 143 us
  waiting for transfers between devices: 18.6 us -> 167 us
  Pallas kernels: 116 us -> 186 us
  starting transfers between devices: 10.7 us -> 45.5 us
    all_to_all x4 -> x3, blocking collectives: 434 us -> 143 us  [exchange(): return lax.all_to_all(values, axis, split_axis=0, concat_axis=0, tiled=True)]
    all_to_all x2 -> x9, waiting for transfers between devices: 18.6 us -> 167 us  [exchange(): return lax.all_to_all(values, axis, split_axis=0, concat_axis=0, tiled=True)]
    pallas_call x2 -> x3, Pallas kernels: 98.9 us -> 137 us  [the longest x2 119 us: dft(): pl.pallas_call(functools.partial(dft_kernel, runs, width, pieces, pairs),...]
    all_to_all x2 -> x9, starting transfers between devices: 10.7 us -> 45.5 us  [exchange(): return lax.all_to_all(values, axis, split_axis=0, concat_axis=0, tiled=True)]
    pallas_call x1 -> x4, Pallas kernels: 17.5 us -> 48.6 us  [on_device(): pl.pallas_call(functools.partial(legendre_kernel, members, lev_rows, band...]
  transfers between devices with their start and end apart: 2 -> 9, of which waited for: 1 -> 8; matrix products, arithmetic and copies ran while one was open for 1% -> 2% of each run, Pallas kernels for 11% -> 19%
where the time goes in v1:
time: 562 us; the launch traced here: 558 us
  Pallas kernels  186 us (33%)
  waiting for transfers between devices  167 us (30%)
  blocking collectives  143 us (25%)
  starting transfers between devices  45.5 us (8%)
  local copies, waits for them, and re-layouts  11.5 us (2%)
    all_to_all x9, waiting for transfers between devices, exchange(): return lax.all_to_all(values, axis, split_axis=0, concat_axis=0, tiled=True)  167 us
    all_to_all x3, blocking collectives, exchange(): return lax.all_to_all(values, axis, split_axis=0, concat_axis=0, tiled=True)  143 us
    pallas_call x2, Pallas kernels, dft(): pl.pallas_call(functools.partial(dft_kernel, runs, width, pieces, pairs),...  119 us
    pallas_call x4, Pallas kernels, on_device(): pl.pallas_call(functools.partial(legendre_kernel, members, lev_rows, band...  48.6 us
    all_to_all x9, starting transfers between devices, exchange(): return lax.all_to_all(values, axis, split_axis=0, concat_axis=0, tiled=True)  45.5 us
    pallas_call x1, Pallas kernels, on_device(): pl.pallas_call(functools.partial(covariance_kernel, part, inner, slots, l...  18.6 us
  transfers between devices with their start and end apart: 9, of which 8 were waited for; matrix products, arithmetic and copies ran while one was open for 2% of the time, Pallas kernels for 19%

profile of v1, /device:TPU:1, one launch (start us, length us, event | category | flops | bytes accessed | tf_op | source)
XLA Modules:
  0.0 558.4 jit_solution(10580616798077111839)
XLA Ops:
  0.0 59.5 %shard_map.91 = (bf16[128,32,384]{2,1,0:T(8,128)(2,1)}, bf16[128,32,384]{2,1,0:T(8,128)(2,1)}) custom-call(f32[384,32,1024]{2,1,0:T(8,128)} %bitcast.27, f32[384,32,1024]{2,1,0:T(8,128)} %bitcast.28, f32[384,32,1024]{2,1,0:T(8,128)} %bitcast.29, f32[384,32,1024]{2,1,0:T(8,128)} %bitcast.30, f32[384,32,1024]{2,1,0:T(8,128)} %bitcast.31, ...), custom_call_target="tpu_custom_call" | custom-call | flops 15000000512 | bytes 65000000 | tf_op jit(solution)/shard_map/pallas_call | solution.py:168
  59.5 42.0 %all_to_all.60.x_ref = bf16[8,2,8,32,384]{4,3,2,1,0:T(8,128)(2,1)} all-to-all(bf16[8,2,8,32,384]{4,3,2,1,0:T(8,128)(2,1)} %bitcast.48), channel_id=1, replica_groups=mesh['lat'=8,'lev'=4] {'lat'}, dimensions={0} | all-to-all | bytes 6291456 | tf_op jit(solution)/shard_map/all_to_all | solution.py:257
  101.5 4.7 all-to-all-start.3
  106.2 59.4 %shard_map.94 = (bf16[128,32,384]{2,1,0:T(8,128)(2,1)}, bf16[128,32,384]{2,1,0:T(8,128)(2,1)}) custom-call(f32[384,32,1024]{2,1,0:T(8,128)} %bitcast.35, f32[384,32,1024]{2,1,0:T(8,128)} %bitcast.36, f32[384,32,1024]{2,1,0:T(8,128)} %bitcast.37, f32[384,32,1024]{2,1,0:T(8,128)} %bitcast.38, f32[384,32,1024]{2,1,0:T(8,128)} %bitcast.39, ...), custom_call_target="tpu_custom_call" | custom-call | flops 15000000512 | bytes 65000000 | tf_op jit(solution)/shard_map/pallas_call | solution.py:168
  165.6 1.6 copy-done
  167.2 4.5 all-to-all-start.5
  171.7 6.6 %copy.16 = bf16[32,8,4,8,256]{4,0,1,2,3:T(8,128)(2,1)} copy(bf16[32,8,4,8,256]{4,3,2,1,0:T(8,128)(2,1)} %bitcast.44) | data formatting | bytes 8388608 | tf_op jit(solution)/shard_map/reshape | solution.py:274
  178.2 27.8 %all-to-all-done.5.x_ref = bf16[8,2,8,32,384]{4,3,2,1,0:T(8,128)(2,1)} async-done(((bf16[8,2,8,32,384]{4,3,2,1,0:T(8,128)(2,1)}), bf16[8,2,8,32,384]{4,3,2,1,0:T(8,128)(2,1)}, u32[]{:S(2)}, u32[]{:S(2)}) %all-to-all-start.5) | async-done | bytes 3145760 | tf_op jit(solution)/shard_map/all_to_all | solution.py:257
  206.1 55.9 %all_to_all.61.l_ref = bf16[8,4,8,32,256]{4,3,2,1,0:T(8,128)(2,1)} all-to-all(bf16[8,4,8,32,256]{4,3,2,1,0:T(8,128)(2,1)} %bitcast.43), channel_id=1, replica_groups=mesh['lat'=8,'lev'=4] {'lat'}, dimensions={0} | all-to-all | bytes 8388608 | tf_op jit(solution)/shard_map/all_to_all | solution.py:257
  262.0 4.8 all-to-all-start.7
  266.8 12.1 %shard_map.92 = bf16[4,576,384]{2,1,0:T(8,128)(2,1)} custom-call(bf16[8,2,8,32,384]{4,3,2,1,0:T(8,128)(2,1)} %all_to_all.60.x_ref, bf16[8,4,8,32,256]{4,3,2,1,0:T(8,128)(2,1)} %all_to_all.61.l_ref), custom_call_target="tpu_custom_call" | custom-call | flops 2000000000 | bytes 12000000 | tf_op jit(solution)/shard_map/pallas_call | solution.py:281
  278.9 22.3 %all-to-all-done.7.x_ref = bf16[8,2,8,32,384]{4,3,2,1,0:T(8,128)(2,1)S(1)} async-done(((bf16[8,2,8,32,384]{4,3,2,1,0:T(8,128)(2,1)}), bf16[8,2,8,32,384]{4,3,2,1,0:T(8,128)(2,1)S(1)}, u32[]{:S(2)}, u32[]{:S(2)}) %all-to-all-start.7) | async-done | bytes 3145760 | tf_op jit(solution)/shard_map/all_to_all | solution.py:257
  301.1 5.2 all-to-all-start.2
  306.3 12.1 %shard_map.93 = bf16[4,576,384]{2,1,0:T(8,128)(2,1)} custom-call(bf16[8,2,8,32,384]{4,3,2,1,0:T(8,128)(2,1)} %copy-done, bf16[8,4,8,32,256]{4,3,2,1,0:T(8,128)(2,1)} %all_to_all.61.l_ref), custom_call_target="tpu_custom_call" | custom-call | flops 2000000000 | bytes 12000000 | tf_op jit(solution)/shard_map/pallas_call | solution.py:281
  318.5 28.7 %all-to-all-done.2.refs_0_ = bf16[4,576,384]{2,1,0:T(8,128)(2,1)} async-done(((bf16[4,576,384]{2,1,0:T(8,128)(2,1)}), bf16[4,576,384]{2,1,0:T(8,128)(2,1)}, u32[]{:S(2)}, u32[]{:S(2)}) %all-to-all-start.2) | async-done | bytes 1769504 | tf_op jit(solution)/shard_map/all_to_all | solution.py:257
  347.2 3.8 all-to-all-start.4
  351.0 12.1 %shard_map.95 = bf16[4,576,384]{2,1,0:T(8,128)(2,1)} custom-call(bf16[8,2,8,32,384]{4,3,2,1,0:T(8,128)(2,1)} %all-to-all-done.5.x_ref, bf16[8,4,8,32,256]{4,3,2,1,0:T(8,128)(2,1)} %all_to_all.61.l_ref), custom_call_target="tpu_custom_call" | custom-call | flops 2000000000 | bytes 12000000 | tf_op jit(solution)/shard_map/pallas_call | solution.py:281
  363.1 28.4 %all-to-all-done.4.refs_1_ = bf16[4,576,384]{2,1,0:T(8,128)(2,1)S(1)} async-done(((bf16[4,576,384]{2,1,0:T(8,128)(2,1)}), bf16[4,576,384]{2,1,0:T(8,128)(2,1)S(1)}, u32[]{:S(2)}, u32[]{:S(2)}) %all-to-all-start.4) | async-done | bytes 1769504 | tf_op jit(solution)/shard_map/all_to_all | solution.py:257
  391.5 3.6 all-to-all-start.6
  395.1 12.2 %shard_map.96 = bf16[4,576,384]{2,1,0:T(8,128)(2,1)} custom-call(bf16[8,2,8,32,384]{4,3,2,1,0:T(8,128)(2,1)} %copy-done.1, bf16[8,4,8,32,256]{4,3,2,1,0:T(8,128)(2,1)} %all_to_all.61.l_ref), custom_call_target="tpu_custom_call" | custom-call | flops 2000000000 | bytes 12000000 | tf_op jit(solution)/shard_map/pallas_call | solution.py:281
  407.3 28.5 %all-to-all-done.6.refs_2_ = bf16[4,576,384]{2,1,0:T(8,128)(2,1)S(1)} async-done(((bf16[4,576,384]{2,1,0:T(8,128)(2,1)}), bf16[4,576,384]{2,1,0:T(8,128)(2,1)S(1)}, u32[]{:S(2)}, u32[]{:S(2)}) %all-to-all-start.6) | async-done | bytes 1769504 | tf_op jit(solution)/shard_map/all_to_all | solution.py:257
  435.8 44.9 %all_to_all.62.refs_3_ = bf16[4,576,384]{2,1,0:T(8,128)(2,1)} all-to-all(bf16[4,576,384]{2,1,0:T(8,128)(2,1)} %shard_map.96), channel_id=1, replica_groups=mesh['lat'=8,'lev'=4] {'lev'}, dimensions={0} | all-to-all | bytes 3538944 | tf_op jit(solution)/shard_map/all_to_all | solution.py:257
  480.7 18.6 %shard_map.97 = bf16[8,8,128,128]{3,2,1,0:T(8,128)(2,1)} custom-call(bf16[4,576,384]{2,1,0:T(8,128)(2,1)} %all-to-all-done.2.refs_0_, bf16[4,576,384]{2,1,0:T(8,128)(2,1)} %copy-done.2, bf16[4,576,384]{2,1,0:T(8,128)(2,1)} %copy-done.3, bf16[4,576,384]{2,1,0:T(8,128)(2,1)} %all_to_all.62.refs_3_), custom_call_target="tpu_custom_call" | custom-call | flops 2000000000 | bytes 16000000 | tf_op jit(solution)/shard_map/pallas_call | solution.py:300
  499.2 6.6 %all-to-all-start.9 = ((bf16[8,8,128,128]{3,2,1,0:T(8,128)(2,1)}), bf16[8,8,128,128]{3,2,1,0:T(8,128)(2,1)S(1)}, u32[]{:S(2)}, u32[]{:S(2)}) async-start(bf16[8,8,128,128]{3,2,1,0:T(8,128)(2,1)} %shard_map.97), calls=%async_computation.9 | async-start | bytes 4194304 | tf_op jit(solution)/shard_map/all_to_all | solution.py:257
  506.2 22.8 %all-to-all-done.9 = bf16[8,8,128,128]{3,2,1,0:T(8,128)(2,1)S(1)} async-done(((bf16[8,8,128,128]{3,2,1,0:T(8,128)(2,1)}), bf16[8,8,128,128]{3,2,1,0:T(8,128)(2,1)S(1)}, u32[]{:S(2)}, u32[]{:S(2)}) %all-to-all-start.9) | async-done | bytes 2097184 | tf_op jit(solution)/shard_map/all_to_all | solution.py:257
  530.2 3.4 all-to-all-start.10
  533.7 5.5 all-to-all-done.10
  539.8 0.9 broadcast_select_fusion
  540.8 9.0 %all-to-all-start.11 = ((bf16[8,8,32,128]{3,2,1,0:T(8,128)(2,1)}), bf16[8,8,32,128]{3,2,1,0:T(8,128)(2,1)S(1)}, u32[]{:S(2)}, u32[]{:S(2)}) async-start(bf16[8,8,32,128]{3,2,1,0:T(8,128)(2,1)} %broadcast_select_fusion), calls=%async_computation.11 | async-start | bytes 1048576 | tf_op jit(solution)/shard_map/all_to_all | solution.py:257
  552.2 1.3 compare_and_fusion.1
  553.5 3.0 all-to-all-done.11
  557.2 1.2 divide_select_fusion
  (27 shorter events, 5.4 us)
Async XLA Ops:
  101.5 64.0 %all-to-all-start.3 = ((bf16[8,2,8,32,384]{4,3,2,1,0:T(8,128)(2,1)}), bf16[8,2,8,32,384]{4,3,2,1,0:T(8,128)(2,1)S(1)}, u32[]{:S(2)}, u32[]{:S(2)}) async-start(bf16[8,2,8,32,384]{4,3,2,1,0:T(8,128)(2,1)} %bitcast.46), calls=%async_computation.3 | async-start | bytes 6291456 | tf_op jit(solution)/shard_map/all_to_all | solution.py:257
  165.6 1.6 copy-start
  167.2 38.9 %all-to-all-start.5 = ((bf16[8,2,8,32,384]{4,3,2,1,0:T(8,128)(2,1)}), bf16[8,2,8,32,384]{4,3,2,1,0:T(8,128)(2,1)}, u32[]{:S(2)}, u32[]{:S(2)}) async-start(bf16[8,2,8,32,384]{4,3,2,1,0:T(8,128)(2,1)} %bitcast.47), calls=%async_computation.5 | async-start | bytes 6291456 | tf_op jit(solution)/shard_map/all_to_all | solution.py:257
  262.0 39.2 %all-to-all-start.7 = ((bf16[8,2,8,32,384]{4,3,2,1,0:T(8,128)(2,1)}), bf16[8,2,8,32,384]{4,3,2,1,0:T(8,128)(2,1)S(1)}, u32[]{:S(2)}, u32[]{:S(2)}) async-start(bf16[8,2,8,32,384]{4,3,2,1,0:T(8,128)(2,1)} %bitcast.45), calls=%async_computation.7 | async-start | bytes 6291456 | tf_op jit(solution)/shard_map/all_to_all | solution.py:257
  301.1 17.3 %copy-start.1 = (bf16[8,2,8,32,384]{4,3,2,1,0:T(8,128)(2,1)}, bf16[8,2,8,32,384]{4,3,2,1,0:T(8,128)(2,1)S(1)}, u32[]{:S(2)}) copy-start(bf16[8,2,8,32,384]{4,3,2,1,0:T(8,128)(2,1)S(1)} %all-to-all-done.7.x_ref) | copy-start | bytes 9437188
  301.1 46.0 %all-to-all-start.2 = ((bf16[4,576,384]{2,1,0:T(8,128)(2,1)}), bf16[4,576,384]{2,1,0:T(8,128)(2,1)}, u32[]{:S(2)}, u32[]{:S(2)}) async-start(bf16[4,576,384]{2,1,0:T(8,128)(2,1)} %shard_map.92), calls=%async_computation.2 | async-start | bytes 3538944 | tf_op jit(solution)/shard_map/all_to_all | solution.py:257
  347.2 44.3 %all-to-all-start.4 = ((bf16[4,576,384]{2,1,0:T(8,128)(2,1)}), bf16[4,576,384]{2,1,0:T(8,128)(2,1)S(1)}, u32[]{:S(2)}, u32[]{:S(2)}) async-start(bf16[4,576,384]{2,1,0:T(8,128)(2,1)} %shard_map.93), calls=%async_computation.4 | async-start | bytes 3538944 | tf_op jit(solution)/shard_map/all_to_all | solution.py:257
  391.5 15.8 %copy-start.2 = (bf16[4,576,384]{2,1,0:T(8,128)(2,1)}, bf16[4,576,384]{2,1,0:T(8,128)(2,1)S(1)}, u32[]{:S(2)}) copy-start(bf16[4,576,384]{2,1,0:T(8,128)(2,1)S(1)} %all-to-all-done.4.refs_1_) | copy-start | bytes 5308420
  391.5 44.3 %all-to-all-start.6 = ((bf16[4,576,384]{2,1,0:T(8,128)(2,1)}), bf16[4,576,384]{2,1,0:T(8,128)(2,1)S(1)}, u32[]{:S(2)}, u32[]{:S(2)}) async-start(bf16[4,576,384]{2,1,0:T(8,128)(2,1)} %shard_map.95), calls=%async_computation.6 | async-start | bytes 3538944 | tf_op jit(solution)/shard_map/all_to_all | solution.py:257
  435.8 44.9 %copy-start.3 = (bf16[4,576,384]{2,1,0:T(8,128)(2,1)}, bf16[4,576,384]{2,1,0:T(8,128)(2,1)S(1)}, u32[]{:S(2)}) copy-start(bf16[4,576,384]{2,1,0:T(8,128)(2,1)S(1)} %all-to-all-done.6.refs_2_) | copy-start | bytes 5308420
  499.2 6.6 %copy-start.4 = (s32[8]{0:T(128)S(1)}, s32[8]{0:T(128)}, u32[]{:S(2)}) copy-start(s32[8]{0:T(128)} %param.11) | copy-start | bytes 100
  499.2 29.8 %all-to-all-start.9 = ((bf16[8,8,128,128]{3,2,1,0:T(8,128)(2,1)}), bf16[8,8,128,128]{3,2,1,0:T(8,128)(2,1)S(1)}, u32[]{:S(2)}, u32[]{:S(2)}) async-start(bf16[8,8,128,128]{3,2,1,0:T(8,128)(2,1)} %shard_map.97), calls=%async_computation.9 | async-start | bytes 4194304 | tf_op jit(solution)/shard_map/all_to_all | solution.py:257
  530.2 9.0 %all-to-all-start.10 = ((bf16[4,8,32,128]{3,2,1,0:T(8,128)(2,1)}), bf16[4,8,32,128]{3,2,1,0:T(8,128)(2,1)S(1)}, u32[]{:S(2)}, u32[]{:S(2)}) async-start(bf16[4,8,32,128]{3,2,1,0:T(8,128)(2,1)} %copy.13), calls=%async_computation.10 | async-start | bytes 524288 | tf_op jit(solution)/shard_map/all_to_all | solution.py:257
  540.8 15.8 %all-to-all-start.11 = ((bf16[8,8,32,128]{3,2,1,0:T(8,128)(2,1)}), bf16[8,8,32,128]{3,2,1,0:T(8,128)(2,1)S(1)}, u32[]{:S(2)}, u32[]{:S(2)}) async-start(bf16[8,8,32,128]{3,2,1,0:T(8,128)(2,1)} %broadcast_select_fusion), calls=%async_computation.11 | async-start | bytes 1048576 | tf_op jit(solution)/shard_map/all_to_all | solution.py:257

commit v2 on v1

v2 whole, which is shorter than its diff:
```python
import functools
import math

import jax
import jax.numpy as jnp
import numpy as np
from jax import lax
from jax.experimental import pallas as pl
from jax.experimental.pallas import tpu as pltpu
from jax.sharding import PartitionSpec as P


def fourier_table(points, modes):
    places = jnp.arange(points, dtype=jnp.int32)
    orders = jnp.arange(modes, dtype=jnp.int32)
    phase = places[:, None] * orders[None, :] % points
    angle = phase.astype(jnp.float32) * (2.0 * math.pi / points)
    factor = points ** (-0.5)
    return jnp.stack([jnp.cos(angle) * factor, -jnp.sin(angle) * factor], axis=2)


def plain_on_device(fields, legendre, owner_counts):
    members, lev_rows, lat_rows, points = fields.shape
    modes = legendre.shape[1]
    lev_count = lax.axis_size("lev")
    owners = owner_counts.shape[0]
    capacity = 2 * modes // owners
    dft_table = fourier_table(points, modes)
    spectra = jnp.einsum("belx,xmc->lmcbe", fields, dft_table, precision=lax.Precision.HIGHEST)
    spectra = spectra.reshape(lat_rows, modes, 2 * members * lev_rows).astype(jnp.bfloat16)
    collected_rows, transform_table_rows = (
        lax.all_to_all(spectra, "lat", split_axis=1, concat_axis=0, tiled=True),
        lax.all_to_all(legendre, "lat", split_axis=1, concat_axis=0, tiled=True),
    )
    wavenumber_rows = jnp.einsum(
        "dez,det->tez", collected_rows, transform_table_rows, preferred_element_type=jnp.float32
    )
    resident_modes = wavenumber_rows.shape[1]
    shaped = wavenumber_rows.reshape(modes, resident_modes, 2, members, lev_rows)
    anomaly = (shaped - jnp.mean(shaped, axis=3, keepdims=True)).astype(jnp.bfloat16)
    anomaly = anomaly.reshape(modes, resident_modes, 2 * members * lev_rows)
    starts = jnp.cumsum(owner_counts) - owner_counts
    offset = jnp.arange(capacity, dtype=jnp.int32)
    active_flag = offset[None, :] < owner_counts[:, None]
    slot_index = jnp.where(active_flag, starts[:, None] + offset[None, :], 0).reshape(-1)
    slotted = jnp.take(anomaly, slot_index, axis=0)
    slotted = jnp.where(active_flag.reshape(-1)[:, None, None], slotted, jnp.zeros_like(slotted))
    slotted = slotted[None]
    received = lax.all_to_all(
        lax.all_to_all(slotted, "lat", split_axis=1, concat_axis=2, tiled=True),
        "lev",
        split_axis=2,
        concat_axis=0,
        tiled=True,
    )
    mode_share = received.shape[2]
    blocks = received.reshape(lev_count, capacity, mode_share, 2 * members, lev_rows)
    partial_value = jnp.einsum(
        "esaql,fsaqk->selfk", blocks, blocks, preferred_element_type=jnp.float32
    )
    partial_value = partial_value.reshape(capacity, lev_count * lev_rows, lev_count * lev_rows)
    summed = lax.psum_scatter(partial_value, "lev", scatter_dimension=1, tiled=True)
    owner = lax.axis_index("lat")
    wavenumber = starts[owner] + offset
    live_count = owner_counts[owner]
    divisor = ((members - 1) * (2 * wavenumber + 2)).astype(jnp.float32)
    scaled = summed / divisor[:, None, None]
    return jnp.where((offset < live_count)[:, None, None], scaled, jnp.zeros_like(scaled))


LANES = 128
SUB = 8
VMEM_LIMIT = 67_043_328


def split_bf16(values):
    high = values.astype(jnp.bfloat16)
    return high, (values - high.astype(jnp.float32)).astype(jnp.bfloat16)


def folded_tables(points, orders):
    tables = []
    for residues, length in (((1, 3), points // 2), ((0,), points // 4), ((2,), points // 4)):
        m = orders[np.isin(orders % 4, residues)]
        angle = 2.0 * np.pi * ((m[:, None] * np.arange(length)[None, :]) % points) / points
        table = np.concatenate([np.cos(angle), -np.sin(angle)]) * points ** -0.5
        table = table.astype(np.float32)
        high = table.astype(jnp.bfloat16)
        low = (table - high.astype(np.float32)).astype(jnp.bfloat16)
        tables.append(np.stack([high, low]))
    return tables


NT = (((1,), (1,)), ((), ()))
TN = (((0,), (0,)), ((), ()))


def block_of(i, j, lat_count):
    return i * lat_count + j if i % 2 == 0 else (i + 1) * lat_count - 1 - j


def main_kernel(size, *refs):
    lat_count, lev_count, members, lev_rows, totals, counts = size
    f_ref, g_ref, odd_ref, zero_ref, two_ref, out_ref = refs[:6]
    blocks = counts
    t_refs = refs[6:6 + blocks]
    (wide, held, sent, got, out_waves, in_waves, joined_ref, cov) = refs[6 + blocks:14 + blocks]
    (f_sem, own_sem, t_send, t_recv, s_send, s_recv, z_send, z_recv) = refs[14 + blocks:]
    me = lax.axis_index("lat")
    depth = lax.axis_index("lev")
    groups = members * lev_rows // LANES
    lat_rows = f_ref.shape[1] * SUB
    pieces = f_ref.shape[3] // LANES
    halves = 2
    eras = lat_rows // (SUB * halves)
    steps = eras * groups
    pairs = 2 * groups
    pack = LANES // lev_rows
    band = SUB * lev_count
    bands = totals // band
    first_band = [i * lat_count // lev_count for i in range(blocks)]
    base = []
    for i in range(blocks):
        base.append(sum(bands - first_band[b] for b in range(i)) - first_band[i])
    lows = [totals - t_refs[i].shape[-1] for i in range(blocks)]

    def lat_peer(offset):
        return lax.rem(me + offset, lat_count)

    def lev_peer(offset):
        return lax.rem(depth + offset, lev_count)

    def fetch_copy(e, half, c):
        l, g = e // groups * halves + half, lax.rem(e, groups)
        return pltpu.make_async_copy(
            f_ref.at[pl.ds(pl.multiple_of(g * LANES, LANES), LANES), l, :, c * LANES:(c + 1) * LANES],
            wide.at[pl.ds((half * pieces + c) * LANES, LANES)],
            f_sem.at[half],
        )

    def fetch_start(e, half):
        for c in range(pieces):
            fetch_copy(e, half, c).start()

    def fetch_wait(half):
        span = wide.at[pl.ds(half * pieces * LANES, pieces * LANES)]
        pltpu.make_async_copy(span, span, f_sem.at[half]).wait()

    def table_source(i, target):
        row = pl.multiple_of(block_of(i, target, lat_count) * SUB, SUB)
        return g_ref.at[:, pl.ds(row, SUB), lows[i]:]

    def table_send(i):
        for offset in range(1, lat_count):
            target = lat_peer(offset)
            pltpu.make_async_remote_copy(
                src_ref=table_source(i, target),
                dst_ref=t_refs[i].at[me],
                send_sem=t_send.at[i],
                recv_sem=t_recv.at[i],
                device_id={"lat": target},
                device_id_type=pl.DeviceIdType.MESH,
            ).start()

    def own_table(i):
        return pltpu.make_async_copy(table_source(i, me), t_refs[i].at[me], own_sem.at[i])

    def own_spectra(i):
        return pltpu.make_async_copy(sent.at[me, i], got.at[i, me], own_sem.at[blocks + i])

    def spectra_send(i, e):
        for offset in range(1, lat_count):
            target = lat_peer(offset)
            pltpu.make_async_remote_copy(
                src_ref=sent.at[target, i, e],
                dst_ref=got.at[i, me, e],
                send_sem=s_send,
                recv_sem=s_recv.at[i],
                device_id={"lat": target},
                device_id_type=pl.DeviceIdType.MESH,
            ).start()

    def waves_send(place):
        for offset in range(1, lev_count):
            target = lev_peer(offset)
            pltpu.make_async_remote_copy(
                src_ref=out_waves.at[place, target],
                dst_ref=in_waves.at[place, depth],
                send_sem=z_send.at[place],
                recv_sem=z_recv.at[place],
                device_id={"lev": target},
                device_id_type=pl.DeviceIdType.MESH,
            ).start()

    def settle(ref, sem):
        pltpu.make_async_copy(ref, ref, sem).wait()

    for half in range(halves):
        fetch_start(0, half)
    barrier = pltpu.get_barrier_semaphore()
    for offset in range(1, lat_count):
        pl.semaphore_signal(
            barrier, inc=1, device_id={"lat": lat_peer(offset)}, device_id_type=pl.DeviceIdType.MESH
        )
    for offset in range(1, lev_count):
        pl.semaphore_signal(
            barrier, inc=1, device_id={"lev": lev_peer(offset)}, device_id_type=pl.DeviceIdType.MESH
        )
    pl.semaphore_wait(barrier, lat_count + lev_count - 2)
    table_send(0)
    for i in range(blocks):
        own_table(i).start()

    rows_view = wide.reshape(wide.shape[0] * SUB, LANES)
    span = SUB * halves
    block_total = lat_count * blocks

    def transform(table_ref, values):
        high, low = split_bf16(values)
        dot = functools.partial(lax.dot_general, dimension_numbers=NT, preferred_element_type=jnp.float32)
        return dot(table_ref[0], high) + (dot(table_ref[1], high) + dot(table_ref[0], low))

    def put(lat, lane, orders, sums):
        count = sums.shape[0] // 2
        for q in range(2):
            for n, order in enumerate(orders):
                row = q * count + n * block_total
                held[q, pl.ds(order * span + lat, block_total, SUB * span), :] = (
                    sums[row:row + block_total, lane:lane + LANES]
                )

    quarter = pieces * LANES // 4
    kinds = [[r for r in range(SUB) if r % 4 in k] for k in ((1, 3), (0,), (2,))]

    def spectra_step(e, carry):
        for half in range(halves):
            fetch_wait(half)

            def pair_step(pair, carry):
                lat = 2 * pair
                values = [
                    jnp.concatenate(
                        [
                            rows_view[pl.ds((half * pieces + c) * LANES * SUB + lat + s, LANES, SUB), :]
                            for s in range(2)
                        ],
                        axis=0,
                    )
                    for c in range(pieces)
                ]
                middle = pieces // 2
                even = jnp.concatenate([u + v for u, v in zip(values[:middle], values[middle:])], axis=1)
                odd = jnp.concatenate([u - v for u, v in zip(values[:middle], values[middle:])], axis=1)
                parts = (
                    transform(odd_ref, odd),
                    transform(zero_ref, even[:, :quarter] + even[:, quarter:]),
                    transform(two_ref, even[:, :quarter] - even[:, quarter:]),
                )
                for s in range(2):
                    for kind, sums in zip(kinds, parts):
                        put(half * SUB + lat + s, s * LANES, kind, sums)
                return carry

            lax.fori_loop(0, SUB // 2, pair_step, 0)

            @pl.when(e < steps - 1)
            def _():
                fetch_start(e + 1, half)

        def emit(target, carry):
            for i in range(blocks):
                for q in range(2):
                    row = pl.multiple_of((target * blocks + i) * SUB * span, SUB * span)
                    block = held[q, pl.ds(row, SUB * span), :].astype(jnp.bfloat16)
                    sent[target, i, e, :, :, q * LANES:(q + 1) * LANES] = block.reshape(SUB, span, LANES)
            return carry

        lax.fori_loop(0, lat_count, emit, 0)
        spectra_send(0, e)

        @pl.when(e > 0)
        def _():
            spectra_send(1, e - 1)

        return carry

    lax.fori_loop(0, steps, spectra_step, 0)
    for i in range(blocks):
        own_spectra(i).start()
    spectra_send(1, steps - 1)
    table_send(1)
    for i in range(2, blocks):
        table_send(i)

        def rest(e, carry):
            spectra_send(i, e)
            return carry

        lax.fori_loop(0, steps, rest, 0)

    def zero(n, carry):
        cov[n] = jnp.zeros(cov.shape[1:], jnp.float32)
        return carry

    lax.fori_loop(0, cov.shape[0], zero, 0)

    depth_rows = lat_count * lat_rows
    table_base = pairs * totals * SUB

    def legendre_sum(i):
        width = totals - lows[i]
        own_table(i).wait()
        settle(t_refs[i].at[pl.ds(0, lat_count - 1)], t_recv.at[i])

        def spread(source, carry):
            for w in range(width // LANES):
                for era in range(eras):
                    at = table_base // SUB + w * depth_rows + (era * lat_count + source) * span
                    wide[pl.ds(at, span)] = t_refs[i][
                        source, era * span:(era + 1) * span, :, w * LANES:(w + 1) * LANES
                    ].astype(jnp.float32)
            return carry

        lax.fori_loop(0, lat_count, spread, 0)
        own_spectra(i).wait()
        settle(got.at[i, pl.ds(0, lat_count - 1)], s_recv.at[i])
        skip = first_band[i] * band - lows[i]

        def one(m, carry):
            table = jnp.concatenate(
                [
                    rows_view[pl.ds(table_base + w * depth_rows * SUB + m, depth_rows, SUB), :]
                    for w in range(width // LANES)
                ],
                axis=1,
            ).astype(jnp.bfloat16)
            waves = []
            for g in range(groups):
                x = jnp.concatenate(
                    [got[i, :, era * groups + g, m].reshape(lat_count * span, 2 * LANES) for era in range(eras)],
                    axis=0,
                )
                full = lax.dot_general(table, x, TN, preferred_element_type=jnp.float32)
                waves.append(full[skip:])
            for q in range(2):
                parts = [w[:, q * LANES:(q + 1) * LANES] for w in waves]
                total = functools.reduce(jnp.add, parts)
                shift = LANES // 2
                while shift >= lev_rows:
                    total = total + pltpu.roll(total, shift, 1)
                    shift //= 2
                mean = total * (1.0 / members)
                for g in range(groups):
                    rows_view[pl.ds((2 * g + q) * totals * SUB + m, parts[g].shape[0], SUB), :] = parts[g] - mean
            return carry

        lax.fori_loop(0, SUB, one, 0)
        start = block_of(i, me, lat_count) // lev_count

        def emit(t, carry):
            place = base[i] + t
            for w in range(pairs):
                for z in range(lev_count):
                    row = w * totals * SUB + ((t - first_band[i]) * lev_count + z) * SUB * SUB
                    block = rows_view[pl.ds(pl.multiple_of(row, SUB), SUB * SUB), :].astype(jnp.bfloat16)
                    out_waves[place, z, :, w * LANES:(w + 1) * LANES] = block
            waves_send(place)
            in_waves[place, depth] = out_waves[place, depth]
            return carry

        lax.fori_loop(start, bands, emit, 0)

    def covariance(i):
        start = block_of(i, me, lat_count) // lev_count

        def one(t, carry):
            place = base[i] + t
            settle(in_waves.at[place, pl.ds(0, lev_count - 1)], z_recv.at[place])
            for w in range(pairs):
                parts = [
                    in_waves[place, v, :, w * LANES:(w + 1) * LANES].astype(jnp.float32)
                    for v in range(lev_count)
                ]
                for s in range(pack):
                    joined = jnp.concatenate([p[:, s * lev_rows:(s + 1) * lev_rows] for p in parts], axis=1)
                    joined_ref[:, w * pack + s] = joined.reshape(SUB, SUB, LANES)

            def multiply(r, carry):
                x = joined_ref[r].reshape(pairs * pack * SUB, LANES).astype(jnp.bfloat16)
                cov[r * bands + t] += lax.dot_general(x, x, TN, preferred_element_type=jnp.float32)
                return carry

            lax.fori_loop(0, SUB, multiply, 0)
            return carry

        lax.fori_loop(start, bands, one, 0)

    for i in range(blocks):
        legendre_sum(i)
        if i >= blocks - 2:
            covariance(i - blocks + 2)
    for i in range(2, blocks):
        covariance(i)

    def finish(n, carry):
        out_ref[n] = cov[n].astype(jnp.bfloat16)
        return carry

    lax.fori_loop(0, cov.shape[0], finish, 0)
    settle(sent.at[pl.ds(0, lat_count - 1)], s_send)
    for i in range(blocks):
        settle(t_refs[i].at[pl.ds(0, lat_count - 1)], t_send.at[i])

        def drain(t, carry):
            place = base[i] + t
            settle(out_waves.at[place, pl.ds(0, lev_count - 1)], z_send.at[place])
            return carry

        lax.fori_loop(block_of(i, me, lat_count) // lev_count, bands, drain, 0)


def main(lat_count, lev_count, fields, legendre):
    members, lev_rows, lat_rows, points = fields.shape
    modes, totals = legendre.shape[1:]
    rows = members * lev_rows
    groups = rows // LANES
    blocks = modes // (SUB * lat_count)
    bands = totals // (SUB * lev_count)
    levels = lev_count * lev_rows
    span = 2 * SUB
    steps = lat_rows // span * groups
    starts = [block_of(i, j, lat_count) * SUB for j in range(lat_count) for i in range(blocks)]
    orders = np.concatenate([np.array(starts) + r for r in range(SUB)])
    tables = [jnp.asarray(t) for t in folded_tables(points, orders)]
    places = sum(bands - i * lat_count // lev_count for i in range(blocks))
    widths = [totals - i * lat_count * SUB // LANES * LANES for i in range(blocks)]
    wide = max(2 * points, 2 * groups * totals + totals // LANES * lat_count * lat_rows)
    size = (lat_count, lev_count, members, lev_rows, totals, blocks)
    vmem = pl.BlockSpec(memory_space=pltpu.VMEM)
    hbm = pl.BlockSpec(memory_space=pl.ANY)
    return pl.pallas_call(
        functools.partial(main_kernel, size),
        out_shape=jax.ShapeDtypeStruct((SUB * bands, levels, levels), jnp.bfloat16),
        in_specs=[hbm, hbm, vmem, vmem, vmem],
        out_specs=vmem,
        scratch_shapes=[pltpu.VMEM((lat_count, lat_rows, SUB, w), jnp.bfloat16) for w in widths]
        + [
            pltpu.VMEM((wide, SUB, LANES), jnp.float32),
            pltpu.VMEM((2, modes * span, LANES), jnp.float32),
            pltpu.VMEM((lat_count, blocks, steps, SUB, span, 2 * LANES), jnp.bfloat16),
            pltpu.VMEM((blocks, lat_count, steps, SUB, span, 2 * LANES), jnp.bfloat16),
            pltpu.VMEM((places, lev_count, SUB * SUB, 2 * rows), jnp.bfloat16),
            pltpu.VMEM((places, lev_count, SUB * SUB, 2 * rows), jnp.bfloat16),
            pltpu.VMEM((SUB, 2 * groups * (LANES // lev_rows), SUB, LANES), jnp.float32),
            pltpu.VMEM((SUB * bands, levels, levels), jnp.float32),
            pltpu.SemaphoreType.DMA((2,)),
            pltpu.SemaphoreType.DMA((2 * blocks,)),
            pltpu.SemaphoreType.DMA((blocks,)),
            pltpu.SemaphoreType.DMA((blocks,)),
            pltpu.SemaphoreType.DMA,
            pltpu.SemaphoreType.DMA((blocks,)),
            pltpu.SemaphoreType.DMA((places,)),
            pltpu.SemaphoreType.DMA((places,)),
        ],
        compiler_params=pltpu.CompilerParams(
            vmem_limit_bytes=VMEM_LIMIT, collective_id=0, has_side_effects=True
        ),
        cost_estimate=pl.CostEstimate(flops=40_000_000_000, bytes_accessed=80_000_000, transcendentals=0),
    )(fields.reshape(rows, lat_rows // SUB, SUB, points), legendre, *tables)


def exchange(values, axis):
    return lax.all_to_all(values, axis, split_axis=0, concat_axis=0, tiled=True)


def on_device(lat_count, lev_count, fields, legendre, owner_counts):
    members, lev_rows, lat_rows, points = fields.shape
    modes, totals = legendre.shape[1:]
    owners = owner_counts.shape[0]
    capacity = 2 * modes // owners
    levels = lev_count * lev_rows
    band = lat_count * lev_count
    slots = modes // band
    partial_value = main(lat_count, lev_count, fields, legendre)
    partial_value = partial_value.reshape(SUB, slots, levels, levels)

    partial_value = exchange(partial_value, "lat")
    summed = jnp.sum(partial_value.astype(jnp.float32), axis=0)
    summed = summed.reshape(slots, lev_count, lev_rows, levels).transpose(1, 0, 2, 3)
    full = exchange(summed.astype(jnp.bfloat16), "lev")
    full = full.transpose(1, 0, 2, 3).reshape(slots * lev_count, lev_rows, levels)

    starts = jnp.cumsum(owner_counts) - owner_counts
    share = capacity // lat_count
    here = lax.axis_index("lat")
    first = starts // lat_count + (starts % lat_count > here).astype(jnp.int32)
    rank = first[:, None] + jnp.arange(share, dtype=jnp.int32)[None, :]
    rank = jnp.minimum(rank, slots * lev_count - 1)
    sent = jnp.take(full, rank.reshape(-1), axis=0).reshape(owners, share, lev_rows, levels)
    sent = exchange(sent, "lat").reshape(lat_count * share, lev_rows, levels)
    offset = jnp.arange(capacity, dtype=jnp.int32)
    wavenumber = starts[here] + offset
    place = wavenumber % lat_count * share + offset // lat_count
    live = offset < owner_counts[here]
    chosen = jnp.take(sent, place, axis=0).astype(jnp.float32)
    divisor = ((members - 1) * (2 * wavenumber + 2)).astype(jnp.float32)
    return jnp.where(live[:, None, None], chosen / divisor[:, None, None], jnp.zeros_like(chosen))


def pick(lat_count, lev_count, fields, legendre, owner_counts):
    members, lev_rows, lat_rows, points = fields.shape
    modes = legendre.shape[1]
    fits = (
        lat_rows % 16 == 0
        and members * lev_rows % LANES == 0
        and lev_rows * lev_count == LANES
        and lat_count == SUB
        and modes % (2 * SUB * lat_count) == 0
        and owner_counts.shape[0] == lat_count
        and 2 * modes // lat_count % lat_count == 0
        and modes % (lat_count * lev_count) == 0
    )
    if fits:
        return on_device(lat_count, lev_count, fields, legendre, owner_counts)
    return plain_on_device(fields, legendre, owner_counts)


def solution(mesh):
    return jax.shard_map(
        functools.partial(pick, mesh.shape["lat"], mesh.shape["lev"]),
        mesh=mesh,
        in_specs=(P(None, "lev", "lat", None), P("lat", None, None), P()),
        out_specs=P("lat", "lev", None),
        check_vma=False,
    )
```

time: 562 us -> 298 us (0.53)
  blocking collectives: 143 us -> 0 us
  waiting for transfers between devices: 167 us -> 31.3 us
  Pallas kernels: 186 us -> 238 us
  starting transfers between devices: 45.5 us -> 16.3 us
  local copies, waits for them, and re-layouts: 11.5 us -> 3.35 us
    all_to_all x3 -> x0, blocking collectives: 143 us -> none  [exchange(): return lax.all_to_all(values, axis, split_axis=0, concat_axis=0, tiled=True)]
    all_to_all x9 -> x3, waiting for transfers between devices: 167 us -> 31.3 us  [exchange(): return lax.all_to_all(values, axis, split_axis=0, concat_axis=0, tiled=True)]
    pallas_call x7 -> x1, Pallas kernels: 186 us -> 238 us  [main(): pl.pallas_call(functools.partial(main_kernel, size), out_shape=jax.ShapeD...]
    all_to_all x9 -> x3, starting transfers between devices: 45.5 us -> 16.3 us  [exchange(): return lax.all_to_all(values, axis, split_axis=0, concat_axis=0, tiled=True)]
    reshape x1 -> x0, local copies, waits for them, and re-layouts: 6.55 us -> none  [on_device(): legendre.reshape(lat_rows, slots, lev_count, lat_count, totals)]
  transfers between devices with their start and end apart: 9 -> 3, of which waited for: 8 -> 3; matrix products, arithmetic and copies ran while one was open for 2% -> 1% of each run, Pallas kernels for 19% -> 0%
where the time goes in v2:
time: 298 us; the launch traced here: 295 us
  Pallas kernels  238 us (80%)
  waiting for transfers between devices  31.3 us (11%)
  starting transfers between devices  16.3 us (5%)
  other arithmetic  5.38 us (2%)
  local copies, waits for them, and re-layouts  3.35 us (1%)
    pallas_call x1, Pallas kernels, main(): pl.pallas_call(functools.partial(main_kernel, size), out_shape=jax.ShapeD...  238 us
    all_to_all x3, waiting for transfers between devices, exchange(): return lax.all_to_all(values, axis, split_axis=0, concat_axis=0, tiled=True)  31.3 us
    all_to_all x3, starting transfers between devices, exchange(): return lax.all_to_all(values, axis, split_axis=0, concat_axis=0, tiled=True)  16.3 us
  transfers between devices with their start and end apart: 3, of which 3 were waited for; matrix products, arithmetic and copies ran while one was open for 1% of the time, Pallas kernels for 0%

profile of v2, /device:TPU:1, one launch (start us, length us, event | category | flops | bytes accessed | tf_op | source)
XLA Modules:
  0.0 294.5 jit_solution(9491898650629963168)
XLA Ops:
  0.0 238.1 %shard_map.64 = bf16[64,128,128]{2,1,0:T(8,128)(2,1)} custom-call(f32[384,4,8,1024]{3,2,1,0:T(8,128)} %bitcast.26, bf16[32,256,256]{2,1,0:T(8,128)(2,1)} %refs_1_.1, bf16[2,256,512]{2,1,0:T(8,128)(2,1)} %constant.107.clone.refs_2_, bf16[2,128,256]{2,1,0:T(8,128)(2,1)} %constant.108.clone.refs_3_, bf16[2,128,256]{2,1,0:T(8,128)(2,1)} %constant.109.clone.refs_4_), custom_call_target="tpu_custom_call" | custom-call | flops 40000000000 | bytes 80000000 | tf_op jit(solution)/shard_map/pallas_call | solution.py:441
  238.2 0.0 copy-start
  238.2 3.6 %all-to-all-start = ((bf16[8,8,128,128]{3,2,1,0:T(8,128)(2,1)}), bf16[8,8,128,128]{3,2,1,0:T(8,128)(2,1)S(1)}, u32[]{:S(2)}, u32[]{:S(2)}) async-start(bf16[8,8,128,128]{3,2,1,0:T(8,128)(2,1)} %bitcast.21), calls=%async_computation | async-start | bytes 4194304 | tf_op jit(solution)/shard_map/all_to_all | solution.py:473
  241.7 0.0 copy-done
  241.8 0.2 reduce-window.9
  242.0 0.1 add_minimum_fusion
  242.0 0.1 min.22
  242.1 22.6 %all-to-all-done = bf16[8,8,128,128]{3,2,1,0:T(8,128)(2,1)S(1)} async-done(((bf16[8,8,128,128]{3,2,1,0:T(8,128)(2,1)}), bf16[8,8,128,128]{3,2,1,0:T(8,128)(2,1)S(1)}, u32[]{:S(2)}, u32[]{:S(2)}) %all-to-all-start) | async-done | bytes 2097184 | tf_op jit(solution)/shard_map/all_to_all | solution.py:473
  264.8 0.4 reduce_sum.12
  265.1 0.7 copy.7
  265.8 3.7 %all-to-all-start.1 = ((bf16[4,8,32,128]{3,2,1,0:T(8,128)(2,1)}), bf16[4,8,32,128]{3,2,1,0:T(8,128)(2,1)S(1)}, u32[]{:S(2)}, u32[]{:S(2)}) async-start(bf16[4,8,32,128]{3,2,1,0:T(8,128)(2,1)} %copy.7), calls=%async_computation.1 | async-start | bytes 524288 | tf_op jit(solution)/shard_map/all_to_all | solution.py:473
  269.6 0.1 compare_and_fusion
  269.7 5.5 %all-to-all-done.1 = bf16[4,8,32,128]{3,2,1,0:T(8,128)(2,1)S(1)} async-done(((bf16[4,8,32,128]{3,2,1,0:T(8,128)(2,1)}), bf16[4,8,32,128]{3,2,1,0:T(8,128)(2,1)S(1)}, u32[]{:S(2)}, u32[]{:S(2)}) %all-to-all-start.1) | async-done | bytes 262176 | tf_op jit(solution)/shard_map/all_to_all | solution.py:473
  275.2 0.7 gather_fusion
  275.9 0.9 broadcast_select_fusion
  276.8 9.0 %all-to-all-start.2 = ((bf16[8,8,32,128]{3,2,1,0:T(8,128)(2,1)}), bf16[8,8,32,128]{3,2,1,0:T(8,128)(2,1)S(1)}, u32[]{:S(2)}, u32[]{:S(2)}) async-start(bf16[8,8,32,128]{3,2,1,0:T(8,128)(2,1)} %broadcast_select_fusion), calls=%async_computation.2 | async-start | bytes 1048576 | tf_op jit(solution)/shard_map/all_to_all | solution.py:473
  285.8 0.6 dynamic_slice.6
  286.4 0.6 dynamic_slice.7
  287.0 0.6 multiply_convert_fusion
  287.7 0.6 fusion.8
  288.3 1.2 compare_and_fusion.1
  289.5 3.1 %all-to-all-done.2 = bf16[8,8,32,128]{3,2,1,0:T(8,128)(2,1)S(1)} async-done(((bf16[8,8,32,128]{3,2,1,0:T(8,128)(2,1)}), bf16[8,8,32,128]{3,2,1,0:T(8,128)(2,1)S(1)}, u32[]{:S(2)}, u32[]{:S(2)}) %all-to-all-start.2) | async-done | bytes 524320 | tf_op jit(solution)/shard_map/all_to_all | solution.py:473
  292.6 0.7 gather_fusion.1
  293.3 1.2 divide_select_fusion
  (5 shorter events, 0.1 us)
Async XLA Ops:
  238.2 3.6 %copy-start = (s32[8]{0:T(128)S(1)}, s32[8]{0:T(128)}, u32[]{:S(2)}) copy-start(s32[8]{0:T(128)} %param.8) | copy-start | bytes 100
  238.2 26.6 %all-to-all-start = ((bf16[8,8,128,128]{3,2,1,0:T(8,128)(2,1)}), bf16[8,8,128,128]{3,2,1,0:T(8,128)(2,1)S(1)}, u32[]{:S(2)}, u32[]{:S(2)}) async-start(bf16[8,8,128,128]{3,2,1,0:T(8,128)(2,1)} %bitcast.21), calls=%async_computation | async-start | bytes 4194304 | tf_op jit(solution)/shard_map/all_to_all | solution.py:473
  265.8 9.4 %all-to-all-start.1 = ((bf16[4,8,32,128]{3,2,1,0:T(8,128)(2,1)}), bf16[4,8,32,128]{3,2,1,0:T(8,128)(2,1)S(1)}, u32[]{:S(2)}, u32[]{:S(2)}) async-start(bf16[4,8,32,128]{3,2,1,0:T(8,128)(2,1)} %copy.7), calls=%async_computation.1 | async-start | bytes 524288 | tf_op jit(solution)/shard_map/all_to_all | solution.py:473
  276.8 15.8 %all-to-all-start.2 = ((bf16[8,8,32,128]{3,2,1,0:T(8,128)(2,1)}), bf16[8,8,32,128]{3,2,1,0:T(8,128)(2,1)S(1)}, u32[]{:S(2)}, u32[]{:S(2)}) async-start(bf16[8,8,32,128]{3,2,1,0:T(8,128)(2,1)} %broadcast_select_fusion), calls=%async_computation.2 | async-start | bytes 1048576 | tf_op jit(solution)/shard_map/all_to_all | solution.py:473

commit v3 on v2

--- a/solution.py
+++ b/solution.py
@@ -101,11 +101,13 @@
 
 def main_kernel(size, *refs):
     lat_count, lev_count, members, lev_rows, totals, counts = size
-    f_ref, g_ref, odd_ref, zero_ref, two_ref, out_ref = refs[:6]
+    c_ref, f_ref, g_ref, odd_ref, zero_ref, two_ref, out_ref = refs[:7]
     blocks = counts
-    t_refs = refs[6:6 + blocks]
-    (wide, held, sent, got, out_waves, in_waves, joined_ref, cov) = refs[6 + blocks:14 + blocks]
-    (f_sem, own_sem, t_send, t_recv, s_send, s_recv, z_send, z_recv) = refs[14 + blocks:]
+    t_refs = refs[7:7 + blocks]
+    (wide, held, sent, got, out_waves, in_waves, joined_ref) = refs[7 + blocks:14 + blocks]
+    (part_out, part_in, rows_out, rows_in, slots_out, slots_in) = refs[14 + blocks:20 + blocks]
+    (f_sem, own_sem, t_send, t_recv, s_send, s_recv, z_send, z_recv) = refs[20 + blocks:28 + blocks]
+    (p_send, p_recv, l_send, l_recv, d_send, d_recv) = refs[28 + blocks:]
     me = lax.axis_index("lat")
     depth = lax.axis_index("lev")
     groups = members * lev_rows // LANES
@@ -298,11 +300,16 @@
 
         lax.fori_loop(0, steps, rest, 0)
 
+    cov = held.reshape(2 * held.shape[1], LANES)
+
+    def cov_rows(r, t):
+        return pl.ds(pl.multiple_of((r * bands + t) * LANES, LANES), LANES)
+
     def zero(n, carry):
-        cov[n] = jnp.zeros(cov.shape[1:], jnp.float32)
+        cov[cov_rows(0, n), :] = jnp.zeros((LANES, LANES), jnp.float32)
         return carry
 
-    lax.fori_loop(0, cov.shape[0], zero, 0)
+    lax.fori_loop(0, SUB * bands, zero, 0)
 
     depth_rows = lat_count * lat_rows
     table_base = pairs * totals * SUB
@@ -387,26 +394,107 @@
 
             def multiply(r, carry):
                 x = joined_ref[r].reshape(pairs * pack * SUB, LANES).astype(jnp.bfloat16)
-                cov[r * bands + t] += lax.dot_general(x, x, TN, preferred_element_type=jnp.float32)
+                cov[cov_rows(r, t), :] += lax.dot_general(x, x, TN, preferred_element_type=jnp.float32)
                 return carry
 
             lax.fori_loop(0, SUB, multiply, 0)
             return carry
 
         lax.fori_loop(start, bands, one, 0)
+
+    def partials(i):
+        def one(t, carry):
+            for r in range(lat_count):
+                part_out[t, r] = cov[cov_rows(r, t), :].astype(jnp.bfloat16)
+            for offset in range(1, lat_count):
+                target = lat_peer(offset)
+                pltpu.make_async_remote_copy(
+                    src_ref=part_out.at[t, target],
+                    dst_ref=part_in.at[t, me],
+                    send_sem=p_send,
+                    recv_sem=p_recv.at[t],
+                    device_id={"lat": target},
+                    device_id_type=pl.DeviceIdType.MESH,
+                ).start()
+            part_in[t, me] = part_out[t, me]
+            return carry
+
+        lax.fori_loop(first_band[i], (first_band + [bands])[i + 1], one, 0)
+
+    def totals_over_lat(low, high):
+        def one(t, carry):
+            settle(part_in.at[t, pl.ds(0, lat_count - 1)], p_recv.at[t])
+            for z in range(lev_count):
+                rows = slice(z * lev_rows, (z + 1) * lev_rows)
+                total = part_in[t, 0, rows].astype(jnp.float32)
+                for source in range(1, lat_count):
+                    total = total + part_in[t, source, rows].astype(jnp.float32)
+                rows_out[z, t] = total.astype(jnp.bfloat16)
+            for offset in range(1, lev_count):
+                target = lev_peer(offset)
+                pltpu.make_async_remote_copy(
+                    src_ref=rows_out.at[target, t],
+                    dst_ref=rows_in.at[depth, t],
+                    send_sem=l_send,
+                    recv_sem=l_recv,
+                    device_id={"lev": target},
+                    device_id_type=pl.DeviceIdType.MESH,
+                ).start()
+            rows_in[depth, t] = rows_out[depth, t]
+            return carry
+
+        lax.fori_loop(low, high, one, 0)
 
     for i in range(blocks):
         legendre_sum(i)
         if i >= blocks - 2:
             covariance(i - blocks + 2)
+            partials(i - blocks + 2)
     for i in range(2, blocks):
         covariance(i)
-
-    def finish(n, carry):
-        out_ref[n] = cov[n].astype(jnp.bfloat16)
+        partials(i)
+    early = first_band[blocks // 2]
+    totals_over_lat(0, early)
+    totals_over_lat(early, bands)
+    settle(rows_in.at[pl.ds(0, lev_count - 1)], l_recv)
+
+    share = slots_out.shape[1]
+    start, mine, count = 0, 0, 0
+    for d in range(lat_count):
+        held_here = c_ref[d]
+        mine = jnp.where(d == me, start, mine)
+        count = jnp.where(d == me, held_here, count)
+        first = start // lat_count + jnp.where(start % lat_count > me, 1, 0)
+        for k in range(share):
+            rank = jnp.minimum(first + k, bands * lev_count - 1)
+            slots_out[d, k] = rows_in[rank % lev_count, rank // lev_count]
+        start = start + held_here
+    for offset in range(1, lat_count):
+        target = lat_peer(offset)
+        pltpu.make_async_remote_copy(
+            src_ref=slots_out.at[target],
+            dst_ref=slots_in.at[me],
+            send_sem=d_send,
+            recv_sem=d_recv,
+            device_id={"lat": target},
+            device_id_type=pl.DeviceIdType.MESH,
+        ).start()
+    slots_in[me] = slots_out[me]
+    settle(slots_in.at[pl.ds(0, lat_count - 1)], d_recv)
+
+    def finish(k, carry):
+        for o in range(lat_count):
+            offset = k * lat_count + o
+            wavenumber = mine + offset
+            divisor = ((members - 1) * (2 * wavenumber + 2)).astype(jnp.float32)
+            chosen = slots_in[wavenumber % lat_count, k].astype(jnp.float32) / divisor
+            out_ref[offset] = jnp.where(offset < count, chosen, jnp.zeros_like(chosen))
         return carry
 
-    lax.fori_loop(0, cov.shape[0], finish, 0)
+    lax.fori_loop(0, share, finish, 0)
+    settle(part_out.at[:, pl.ds(0, lat_count - 1)], p_send)
+    settle(rows_out.at[pl.ds(0, lev_count - 1)], l_send)
+    settle(slots_out.at[pl.ds(0, lat_count - 1)], d_send)
     settle(sent.at[pl.ds(0, lat_count - 1)], s_send)
     for i in range(blocks):
         settle(t_refs[i].at[pl.ds(0, lat_count - 1)], t_send.at[i])
@@ -419,7 +507,7 @@
         lax.fori_loop(block_of(i, me, lat_count) // lev_count, bands, drain, 0)
 
 
-def main(lat_count, lev_count, fields, legendre):
+def on_device(lat_count, lev_count, fields, legendre, owner_counts):
     members, lev_rows, lat_rows, points = fields.shape
     modes, totals = legendre.shape[1:]
     rows = members * lev_rows
@@ -438,10 +526,13 @@
     size = (lat_count, lev_count, members, lev_rows, totals, blocks)
     vmem = pl.BlockSpec(memory_space=pltpu.VMEM)
     hbm = pl.BlockSpec(memory_space=pl.ANY)
+    smem = pl.BlockSpec(memory_space=pltpu.SMEM)
+    capacity = 2 * modes // owner_counts.shape[0]
+    share = capacity // lat_count
     return pl.pallas_call(
         functools.partial(main_kernel, size),
-        out_shape=jax.ShapeDtypeStruct((SUB * bands, levels, levels), jnp.bfloat16),
-        in_specs=[hbm, hbm, vmem, vmem, vmem],
+        out_shape=jax.ShapeDtypeStruct((capacity, lev_rows, levels), jnp.float32),
+        in_specs=[smem, hbm, hbm, vmem, vmem, vmem],
         out_specs=vmem,
         scratch_shapes=[pltpu.VMEM((lat_count, lat_rows, SUB, w), jnp.bfloat16) for w in widths]
         + [
@@ -452,7 +543,12 @@
             pltpu.VMEM((places, lev_count, SUB * SUB, 2 * rows), jnp.bfloat16),
             pltpu.VMEM((places, lev_count, SUB * SUB, 2 * rows), jnp.bfloat16),
             pltpu.VMEM((SUB, 2 * groups * (LANES // lev_rows), SUB, LANES), jnp.float32),
-            pltpu.VMEM((SUB * bands, levels, levels), jnp.float32),
+            pltpu.VMEM((bands, lat_count, levels, levels), jnp.bfloat16),
+            pltpu.VMEM((bands, lat_count, levels, levels), jnp.bfloat16),
+            pltpu.VMEM((lev_count, bands, lev_rows, levels), jnp.bfloat16),
+            pltpu.VMEM((lev_count, bands, lev_rows, levels), jnp.bfloat16),
+            pltpu.VMEM((lat_count, share, lev_rows, levels), jnp.bfloat16),
+            pltpu.VMEM((lat_count, share, lev_rows, levels), jnp.bfloat16),
             pltpu.SemaphoreType.DMA((2,)),
             pltpu.SemaphoreType.DMA((2 * blocks,)),
             pltpu.SemaphoreType.DMA((blocks,)),
@@ -461,50 +557,18 @@
             pltpu.SemaphoreType.DMA((blocks,)),
             pltpu.SemaphoreType.DMA((places,)),
             pltpu.SemaphoreType.DMA((places,)),
+            pltpu.SemaphoreType.DMA,
+            pltpu.SemaphoreType.DMA((bands,)),
+            pltpu.SemaphoreType.DMA,
+            pltpu.SemaphoreType.DMA,
+            pltpu.SemaphoreType.DMA,
+            pltpu.SemaphoreType.DMA,
         ],
         compiler_params=pltpu.CompilerParams(
             vmem_limit_bytes=VMEM_LIMIT, collective_id=0, has_side_effects=True
         ),
         cost_estimate=pl.CostEstimate(flops=40_000_000_000, bytes_accessed=80_000_000, transcendentals=0),
-    )(fields.reshape(rows, lat_rows // SUB, SUB, points), legendre, *tables)
-
-
-def exchange(values, axis):
-    return lax.all_to_all(values, axis, split_axis=0, concat_axis=0, tiled=True)
-
-
-def on_device(lat_count, lev_count, fields, legendre, owner_counts):
-    members, lev_rows, lat_rows, points = fields.shape
-    modes, totals = legendre.shape[1:]
-    owners = owner_counts.shape[0]
-    capacity = 2 * modes // owners
-    levels = lev_count * lev_rows
-    band = lat_count * lev_count
-    slots = modes // band
-    partial_value = main(lat_count, lev_count, fields, legendre)
-    partial_value = partial_value.reshape(SUB, slots, levels, levels)
-
-    partial_value = exchange(partial_value, "lat")
-    summed = jnp.sum(partial_value.astype(jnp.float32), axis=0)
-    summed = summed.reshape(slots, lev_count, lev_rows, levels).transpose(1, 0, 2, 3)
-    full = exchange(summed.astype(jnp.bfloat16), "lev")
-    full = full.transpose(1, 0, 2, 3).reshape(slots * lev_count, lev_rows, levels)
-
-    starts = jnp.cumsum(owner_counts) - owner_counts
-    share = capacity // lat_count
-    here = lax.axis_index("lat")
-    first = starts // lat_count + (starts % lat_count > here).astype(jnp.int32)
-    rank = first[:, None] + jnp.arange(share, dtype=jnp.int32)[None, :]
-    rank = jnp.minimum(rank, slots * lev_count - 1)
-    sent = jnp.take(full, rank.reshape(-1), axis=0).reshape(owners, share, lev_rows, levels)
-    sent = exchange(sent, "lat").reshape(lat_count * share, lev_rows, levels)
-    offset = jnp.arange(capacity, dtype=jnp.int32)
-    wavenumber = starts[here] + offset
-    place = wavenumber % lat_count * share + offset // lat_count
-    live = offset < owner_counts[here]
-    chosen = jnp.take(sent, place, axis=0).astype(jnp.float32)
-    divisor = ((members - 1) * (2 * wavenumber + 2)).astype(jnp.float32)
-    return jnp.where(live[:, None, None], chosen / divisor[:, None, None], jnp.zeros_like(chosen))
+    )(owner_counts, fields.reshape(rows, lat_rows // SUB, SUB, points), legendre, *tables)
 
 
 def pick(lat_count, lev_count, fields, legendre, owner_counts):
@@ -518,6 +582,7 @@
         and modes % (2 * SUB * lat_count) == 0
         and owner_counts.shape[0] == lat_count
         and 2 * modes // lat_count % lat_count == 0
+        and legendre.shape[2] <= 2 * modes
         and modes % (lat_count * lev_count) == 0
     )
     if fits:

time: 298 us -> 261 us (0.88); the launches traced: 295 us -> 261 us
  waiting for transfers between devices: 31.3 us -> 0 us
  Pallas kernels: 238 us -> 259 us
  starting transfers between devices: 16.3 us -> 0 us
  other arithmetic: 5.38 us -> 0 us
    all_to_all x3 -> x0, waiting for transfers between devices: 31.3 us -> none  [exchange(): return lax.all_to_all(values, axis, split_axis=0, concat_axis=0, tiled=True)]
    pallas_call x1, Pallas kernels: 238 us -> 259 us  [on_device(): pl.pallas_call(functools.partial(main_kernel, size), out_shape=jax.ShapeD...]
    all_to_all x3 -> x0, starting transfers between devices: 16.3 us -> none  [exchange(): return lax.all_to_all(values, axis, split_axis=0, concat_axis=0, tiled=True)]
  transfers between devices with their start and end apart: 3 -> 0, of which waited for: 3 -> 0; matrix products, arithmetic and copies ran while one was open for 1% -> 0% of each run, Pallas kernels for 0% -> 0%
where the time goes in v3:
time: 261 us
  Pallas kernels  259 us (99%)
    pallas_call x1, Pallas kernels, on_device(): pl.pallas_call(functools.partial(main_kernel, size), out_shape=jax.ShapeD...  259 us

profile of v3, /device:TPU:1, one launch (start us, length us, event | category | flops | bytes accessed | tf_op | source)
XLA Modules:
  0.0 261.2 jit_solution(12801647960965966106)
XLA Ops:
  0.0 259.0 %shard_map.64 = f32[64,32,128]{2,1,0:T(8,128)} custom-call(s32[8]{0:T(128)} %refs_0_.1, f32[384,4,8,1024]{3,2,1,0:T(8,128)} %bitcast.1, bf16[32,256,256]{2,1,0:T(8,128)(2,1)} %refs_2_.1, bf16[2,256,512]{2,1,0:T(8,128)(2,1)} %constant.6.clone.refs_3_, bf16[2,128,256]{2,1,0:T(8,128)(2,1)} %constant.7.clone.refs_4_, bf16[2,128,256]{2,1,0:T(8,128)(2,1)} %constant.8.clone.refs_5_), custom_call_target="tpu_custom_call" | custom-call | flops 40000000000 | bytes 80000000 | tf_op jit(solution)/shard_map/pallas_call | solution.py:532
  259.0 2.3 copy.8

commit v4 on v3

--- a/solution.py
+++ b/solution.py
@@ -220,19 +220,13 @@
     def transform(table_ref, values):
         high, low = split_bf16(values)
         dot = functools.partial(lax.dot_general, dimension_numbers=NT, preferred_element_type=jnp.float32)
-        return dot(table_ref[0], high) + (dot(table_ref[1], high) + dot(table_ref[0], low))
-
-    def put(lat, lane, orders, sums):
-        count = sums.shape[0] // 2
-        for q in range(2):
-            for n, order in enumerate(orders):
-                row = q * count + n * block_total
-                held[q, pl.ds(order * span + lat, block_total, SUB * span), :] = (
-                    sums[row:row + block_total, lane:lane + LANES]
-                )
+        count = table_ref.shape[1]
+        both = dot(table_ref[...].reshape(2 * count, table_ref.shape[2]), high)
+        return both[:count] + (both[count:] + dot(table_ref[0], low))
 
     quarter = pieces * LANES // 4
     kinds = [[r for r in range(SUB) if r % 4 in k] for k in ((1, 3), (0,), (2,))]
+    kind_rows = [2 * block_total * sum(len(k) for k in kinds[:n]) for n in range(len(kinds))]
 
     def spectra_step(e, carry):
         for half in range(halves):
@@ -259,8 +253,10 @@
                     transform(two_ref, even[:, :quarter] - even[:, quarter:]),
                 )
                 for s in range(2):
-                    for kind, sums in zip(kinds, parts):
-                        put(half * SUB + lat + s, s * LANES, kind, sums)
+                    for row, sums in zip(kind_rows, parts):
+                        held[half, pl.ds(row * SUB + lat + s, sums.shape[0], SUB), :] = (
+                            sums[:, s * LANES:(s + 1) * LANES]
+                        )
                 return carry
 
             lax.fori_loop(0, SUB // 2, pair_step, 0)
@@ -271,27 +267,23 @@
 
         def emit(target, carry):
             for i in range(blocks):
-                for q in range(2):
-                    row = pl.multiple_of((target * blocks + i) * SUB * span, SUB * span)
-                    block = held[q, pl.ds(row, SUB * span), :].astype(jnp.bfloat16)
-                    sent[target, i, e, :, :, q * LANES:(q + 1) * LANES] = block.reshape(SUB, span, LANES)
+                for first, kind in zip(kind_rows, kinds):
+                    for n, order in enumerate(kind):
+                        for q in range(2):
+                            row = first + (q * len(kind) + n) * block_total + target * blocks + i
+                            rows = pl.ds(pl.multiple_of(row * SUB, SUB), SUB)
+                            block = jnp.concatenate([held[half, rows, :] for half in range(halves)], axis=0)
+                            sent[target, i, e, order, :, q * LANES:(q + 1) * LANES] = block.astype(jnp.bfloat16)
             return carry
 
         lax.fori_loop(0, lat_count, emit, 0)
         spectra_send(0, e)
-
-        @pl.when(e > 0)
-        def _():
-            spectra_send(1, e - 1)
-
         return carry
 
     lax.fori_loop(0, steps, spectra_step, 0)
     for i in range(blocks):
         own_spectra(i).start()
-    spectra_send(1, steps - 1)
-    table_send(1)
-    for i in range(2, blocks):
+    for i in range(1, blocks):
         table_send(i)
 
         def rest(e, carry):

time: 261 us -> 238 us (0.912)
  Pallas kernels: 259 us -> 236 us
    pallas_call x1, Pallas kernels: 259 us -> 236 us  [on_device(): pl.pallas_call(functools.partial(main_kernel, size), out_shape=jax.ShapeD...]
where the time goes in v4:
time: 238 us
  Pallas kernels  236 us (99%)
    pallas_call x1, Pallas kernels, on_device(): pl.pallas_call(functools.partial(main_kernel, size), out_shape=jax.ShapeD...  236 us

profile of v4, /device:TPU:1, one launch (start us, length us, event | category | flops | bytes accessed | tf_op | source)
XLA Modules:
  0.0 237.9 jit_solution(12738218964966840151)
XLA Ops:
  0.0 235.7 %shard_map.64 = f32[64,32,128]{2,1,0:T(8,128)} custom-call(s32[8]{0:T(128)} %refs_0_.1, f32[384,4,8,1024]{3,2,1,0:T(8,128)} %bitcast.1, bf16[32,256,256]{2,1,0:T(8,128)(2,1)} %refs_2_.1, bf16[2,256,512]{2,1,0:T(8,128)(2,1)} %constant.6.clone.refs_3_, bf16[2,128,256]{2,1,0:T(8,128)(2,1)} %constant.7.clone.refs_4_, bf16[2,128,256]{2,1,0:T(8,128)(2,1)} %constant.8.clone.refs_5_), custom_call_target="tpu_custom_call" | custom-call | flops 40000000000 | bytes 80000000 | tf_op jit(solution)/shard_map/pallas_call | solution.py:524
  235.7 2.3 copy.8

commit v5 on v4

--- a/solution.py
+++ b/solution.py
@@ -125,6 +125,9 @@
     for i in range(blocks):
         base.append(sum(bands - first_band[b] for b in range(i)) - first_band[i])
     lows = [totals - t_refs[i].shape[-1] for i in range(blocks)]
+    columns = [[(low, totals, i)] for i, low in enumerate(lows)]
+    if totals - lows[0] > LANES:
+        columns[0] = [(totals - LANES, totals, 0), (lows[0], totals - LANES, blocks)]
 
     def lat_peer(offset):
         return lax.rem(me + offset, lat_count)
@@ -148,24 +151,25 @@
         span = wide.at[pl.ds(half * pieces * LANES, pieces * LANES)]
         pltpu.make_async_copy(span, span, f_sem.at[half]).wait()
 
-    def table_source(i, target):
+    def table_source(i, target, start, stop):
         row = pl.multiple_of(block_of(i, target, lat_count) * SUB, SUB)
-        return g_ref.at[:, pl.ds(row, SUB), lows[i]:]
-
-    def table_send(i):
+        return g_ref.at[:, pl.ds(row, SUB), start:stop]
+
+    def table_send(i, part):
+        start, stop, sem = part
         for offset in range(1, lat_count):
             target = lat_peer(offset)
             pltpu.make_async_remote_copy(
-                src_ref=table_source(i, target),
-                dst_ref=t_refs[i].at[me],
-                send_sem=t_send.at[i],
-                recv_sem=t_recv.at[i],
+                src_ref=table_source(i, target, start, stop),
+                dst_ref=t_refs[i].at[me, :, :, start - lows[i]:stop - lows[i]],
+                send_sem=t_send.at[sem],
+                recv_sem=t_recv.at[sem],
                 device_id={"lat": target},
                 device_id_type=pl.DeviceIdType.MESH,
             ).start()
 
     def own_table(i):
-        return pltpu.make_async_copy(table_source(i, me), t_refs[i].at[me], own_sem.at[i])
+        return pltpu.make_async_copy(table_source(i, me, lows[i], totals), t_refs[i].at[me], own_sem.at[i])
 
     def own_spectra(i):
         return pltpu.make_async_copy(sent.at[me, i], got.at[i, me], own_sem.at[blocks + i])
@@ -182,17 +186,23 @@
                 device_id_type=pl.DeviceIdType.MESH,
             ).start()
 
-    def waves_send(place):
+    def waves_copy(place, offset):
+        target = lev_peer(offset)
+        return pltpu.make_async_remote_copy(
+            src_ref=out_waves.at[place, target],
+            dst_ref=in_waves.at[place, depth],
+            send_sem=z_send.at[place, offset - 1],
+            recv_sem=z_recv.at[place],
+            device_id={"lev": target},
+            device_id_type=pl.DeviceIdType.MESH,
+        )
+
+    def for_waves(i, t, act):
         for offset in range(1, lev_count):
-            target = lev_peer(offset)
-            pltpu.make_async_remote_copy(
-                src_ref=out_waves.at[place, target],
-                dst_ref=in_waves.at[place, depth],
-                send_sem=z_send.at[place],
-                recv_sem=z_recv.at[place],
-                device_id={"lev": target},
-                device_id_type=pl.DeviceIdType.MESH,
-            ).start()
+
+            @pl.when(t * lev_count + lev_peer(offset) >= block_of(i, me, lat_count))
+            def _():
+                act(waves_copy(base[i] + t, offset))
 
     def settle(ref, sem):
         pltpu.make_async_copy(ref, ref, sem).wait()
@@ -209,7 +219,7 @@
             barrier, inc=1, device_id={"lev": lev_peer(offset)}, device_id_type=pl.DeviceIdType.MESH
         )
     pl.semaphore_wait(barrier, lat_count + lev_count - 2)
-    table_send(0)
+    table_send(0, columns[0][0])
     for i in range(blocks):
         own_table(i).start()
 
@@ -283,8 +293,11 @@
     lax.fori_loop(0, steps, spectra_step, 0)
     for i in range(blocks):
         own_spectra(i).start()
+    for part in columns[0][1:]:
+        table_send(0, part)
     for i in range(1, blocks):
-        table_send(i)
+        for part in columns[i]:
+            table_send(i, part)
 
         def rest(e, carry):
             spectra_send(i, e)
@@ -307,23 +320,31 @@
     table_base = pairs * totals * SUB
 
     def legendre_sum(i):
-        width = totals - lows[i]
         own_table(i).wait()
-        settle(t_refs[i].at[pl.ds(0, lat_count - 1)], t_recv.at[i])
+        for n, part in enumerate(columns[i]):
+            legendre_part(i, part, n == 0)
+
+    def legendre_part(i, part, first):
+        left, right, sem = part
+        width = right - left
+        low = left - lows[i]
+        settle(t_refs[i].at[pl.ds(0, lat_count - 1), :, :, low:low + width], t_recv.at[sem])
 
         def spread(source, carry):
             for w in range(width // LANES):
                 for era in range(eras):
                     at = table_base // SUB + w * depth_rows + (era * lat_count + source) * span
                     wide[pl.ds(at, span)] = t_refs[i][
-                        source, era * span:(era + 1) * span, :, w * LANES:(w + 1) * LANES
+                        source, era * span:(era + 1) * span, :, low + w * LANES:low + (w + 1) * LANES
                     ].astype(jnp.float32)
             return carry
 
         lax.fori_loop(0, lat_count, spread, 0)
-        own_spectra(i).wait()
-        settle(got.at[i, pl.ds(0, lat_count - 1)], s_recv.at[i])
-        skip = first_band[i] * band - lows[i]
+        if first:
+            own_spectra(i).wait()
+            settle(got.at[i, pl.ds(0, lat_count - 1)], s_recv.at[i])
+        skip = max(first_band[i] * band - left, 0)
+        place_row = (left + skip - first_band[i] * band) * SUB
 
         def one(m, carry):
             table = jnp.concatenate(
@@ -350,11 +371,12 @@
                     shift //= 2
                 mean = total * (1.0 / members)
                 for g in range(groups):
-                    rows_view[pl.ds((2 * g + q) * totals * SUB + m, parts[g].shape[0], SUB), :] = parts[g] - mean
+                    rows = pl.ds((2 * g + q) * totals * SUB + place_row + m, parts[g].shape[0], SUB)
+                    rows_view[rows, :] = parts[g] - mean
             return carry
 
         lax.fori_loop(0, SUB, one, 0)
-        start = block_of(i, me, lat_count) // lev_count
+        start = jnp.maximum(block_of(i, me, lat_count) // lev_count, left // band)
 
         def emit(t, carry):
             place = base[i] + t
@@ -363,14 +385,14 @@
                     row = w * totals * SUB + ((t - first_band[i]) * lev_count + z) * SUB * SUB
                     block = rows_view[pl.ds(pl.multiple_of(row, SUB), SUB * SUB), :].astype(jnp.bfloat16)
                     out_waves[place, z, :, w * LANES:(w + 1) * LANES] = block
-            waves_send(place)
+            for_waves(i, t, lambda copy: copy.start())
             in_waves[place, depth] = out_waves[place, depth]
             return carry
 
-        lax.fori_loop(start, bands, emit, 0)
+        lax.fori_loop(start, right // band, emit, 0)
 
     def covariance(i):
-        start = block_of(i, me, lat_count) // lev_count
+        start = (block_of(i, me, lat_count) + lev_count - 1 - depth) // lev_count
 
         def one(t, carry):
             place = base[i] + t
@@ -489,11 +511,12 @@
     settle(slots_out.at[pl.ds(0, lat_count - 1)], d_send)
     settle(sent.at[pl.ds(0, lat_count - 1)], s_send)
     for i in range(blocks):
-        settle(t_refs[i].at[pl.ds(0, lat_count - 1)], t_send.at[i])
+        for left, right, sem in columns[i]:
+            part = t_refs[i].at[pl.ds(0, lat_count - 1), :, :, left - lows[i]:right - lows[i]]
+            settle(part, t_send.at[sem])
 
         def drain(t, carry):
-            place = base[i] + t
-            settle(out_waves.at[place, pl.ds(0, lev_count - 1)], z_send.at[place])
+            for_waves(i, t, lambda copy: copy.wait_send())
             return carry
 
         lax.fori_loop(block_of(i, me, lat_count) // lev_count, bands, drain, 0)
@@ -543,11 +566,11 @@
             pltpu.VMEM((lat_count, share, lev_rows, levels), jnp.bfloat16),
             pltpu.SemaphoreType.DMA((2,)),
             pltpu.SemaphoreType.DMA((2 * blocks,)),
-            pltpu.SemaphoreType.DMA((blocks,)),
-            pltpu.SemaphoreType.DMA((blocks,)),
+            pltpu.SemaphoreType.DMA((blocks + 1,)),
+            pltpu.SemaphoreType.DMA((blocks + 1,)),
             pltpu.SemaphoreType.DMA,
             pltpu.SemaphoreType.DMA((blocks,)),
-            pltpu.SemaphoreType.DMA((places,)),
+            pltpu.SemaphoreType.DMA((places, lev_count - 1)),
             pltpu.SemaphoreType.DMA((places,)),
             pltpu.SemaphoreType.DMA,
             pltpu.SemaphoreType.DMA((bands,)),

time: 238 us -> 233 us (0.979)
  Pallas kernels: 236 us -> 231 us
    pallas_call x1, Pallas kernels: 236 us -> 231 us  [on_device(): pl.pallas_call(functools.partial(main_kernel, size), out_shape=jax.ShapeD...]
where the time goes in v5:
time: 233 us
  Pallas kernels  231 us (99%)
    pallas_call x1, Pallas kernels, on_device(): pl.pallas_call(functools.partial(main_kernel, size), out_shape=jax.ShapeD...  231 us

profile of v5, /device:TPU:1, one launch (start us, length us, event | category | flops | bytes accessed | tf_op | source)
XLA Modules:
  0.0 233.3 jit_solution(10870184846179965904)
XLA Ops:
  0.0 231.0 %shard_map.64 = f32[64,32,128]{2,1,0:T(8,128)} custom-call(s32[8]{0:T(128)} %refs_0_.1, f32[384,4,8,1024]{3,2,1,0:T(8,128)} %bitcast.1, bf16[32,256,256]{2,1,0:T(8,128)(2,1)} %refs_2_.1, bf16[2,256,512]{2,1,0:T(8,128)(2,1)} %constant.6.clone.refs_3_, bf16[2,128,256]{2,1,0:T(8,128)(2,1)} %constant.7.clone.refs_4_, bf16[2,128,256]{2,1,0:T(8,128)(2,1)} %constant.8.clone.refs_5_), custom_call_target="tpu_custom_call" | custom-call | flops 40000000000 | bytes 80000000 | tf_op jit(solution)/shard_map/pallas_call | solution.py:547
  231.0 2.3 copy.8

commit v6 on v5

--- a/solution.py
+++ b/solution.py
@@ -391,7 +391,7 @@
 
         lax.fori_loop(start, right // band, emit, 0)
 
-    def covariance(i):
+    def covariance(i, low, high):
         start = (block_of(i, me, lat_count) + lev_count - 1 - depth) // lev_count
 
         def one(t, carry):
@@ -406,17 +406,19 @@
                     joined = jnp.concatenate([p[:, s * lev_rows:(s + 1) * lev_rows] for p in parts], axis=1)
                     joined_ref[:, w * pack + s] = joined.reshape(SUB, SUB, LANES)
 
-            def multiply(r, carry):
-                x = joined_ref[r].reshape(pairs * pack * SUB, LANES).astype(jnp.bfloat16)
-                cov[cov_rows(r, t), :] += lax.dot_general(x, x, TN, preferred_element_type=jnp.float32)
+            def multiply(n, carry):
+                for s in range(SUB // 2):
+                    r = n * (SUB // 2) + s
+                    x = joined_ref[r].reshape(pairs * pack * SUB, LANES).astype(jnp.bfloat16)
+                    cov[cov_rows(r, t), :] += lax.dot_general(x, x, TN, preferred_element_type=jnp.float32)
                 return carry
 
-            lax.fori_loop(0, SUB, multiply, 0)
-            return carry
-
-        lax.fori_loop(start, bands, one, 0)
-
-    def partials(i):
+            lax.fori_loop(0, 2, multiply, 0)
+            return carry
+
+        lax.fori_loop(jnp.maximum(start, low), high, one, 0)
+
+    def partials(low, high):
         def one(t, carry):
             for r in range(lat_count):
                 part_out[t, r] = cov[cov_rows(r, t), :].astype(jnp.bfloat16)
@@ -433,7 +435,7 @@
             part_in[t, me] = part_out[t, me]
             return carry
 
-        lax.fori_loop(first_band[i], (first_band + [bands])[i + 1], one, 0)
+        lax.fori_loop(low, high, one, 0)
 
     def totals_over_lat(low, high):
         def one(t, carry):
@@ -461,12 +463,14 @@
 
     for i in range(blocks):
         legendre_sum(i)
-        if i >= blocks - 2:
-            covariance(i - blocks + 2)
-            partials(i - blocks + 2)
-    for i in range(2, blocks):
-        covariance(i)
-        partials(i)
+        if i > 0 and i < blocks - 1:
+            covariance(i - 1, 0, bands)
+            partials(first_band[i - 1], first_band[i])
+    covariance(blocks - 2, 0, bands)
+    partials(first_band[blocks - 2], first_band[blocks - 1])
+    for t in range(first_band[blocks - 1], bands):
+        covariance(blocks - 1, t, t + 1)
+        partials(t, t + 1)
     early = first_band[blocks // 2]
     totals_over_lat(0, early)
     totals_over_lat(early, bands)

time: 233 us -> 231 us (level)
  no operation moved by 1% of the time
where the time goes in v6:
time: 231 us
  Pallas kernels  229 us (99%)
    pallas_call x1, Pallas kernels, on_device(): pl.pallas_call(functools.partial(main_kernel, size), out_shape=jax.ShapeD...  229 us

profile of v6, /device:TPU:1, one launch (start us, length us, event | category | flops | bytes accessed | tf_op | source)
XLA Modules:
  0.0 231.2 jit_solution(9783672841665599842)
XLA Ops:
  0.0 228.9 %shard_map.64 = f32[64,32,128]{2,1,0:T(8,128)} custom-call(s32[8]{0:T(128)} %refs_0_.1, f32[384,4,8,1024]{3,2,1,0:T(8,128)} %bitcast.1, bf16[32,256,256]{2,1,0:T(8,128)(2,1)} %refs_2_.1, bf16[2,256,512]{2,1,0:T(8,128)(2,1)} %constant.6.clone.refs_3_, bf16[2,128,256]{2,1,0:T(8,128)(2,1)} %constant.7.clone.refs_4_, bf16[2,128,256]{2,1,0:T(8,128)(2,1)} %constant.8.clone.refs_5_), custom_call_target="tpu_custom_call" | custom-call | flops 40000000000 | bytes 80000000 | tf_op jit(solution)/shard_map/pallas_call | solution.py:551
  229.0 2.3 copy.8

commit v7 on v6

--- a/solution.py
+++ b/solution.py
@@ -107,7 +107,7 @@
     (wide, held, sent, got, out_waves, in_waves, joined_ref) = refs[7 + blocks:14 + blocks]
     (part_out, part_in, rows_out, rows_in, slots_out, slots_in) = refs[14 + blocks:20 + blocks]
     (f_sem, own_sem, t_send, t_recv, s_send, s_recv, z_send, z_recv) = refs[20 + blocks:28 + blocks]
-    (p_send, p_recv, l_send, l_recv, d_send, d_recv) = refs[28 + blocks:]
+    (p_send, p_recv, l_send, l_recv, d_send, d_recv, w_send, w_recv) = refs[28 + blocks:]
     me = lax.axis_index("lat")
     depth = lax.axis_index("lev")
     groups = members * lev_rows // LANES
@@ -128,6 +128,8 @@
     columns = [[(low, totals, i)] for i, low in enumerate(lows)]
     if totals - lows[0] > LANES:
         columns[0] = [(totals - LANES, totals, 0), (lows[0], totals - LANES, blocks)]
+    shared = (1, blocks)
+    portion = lat_rows // lev_count
 
     def lat_peer(offset):
         return lax.rem(me + offset, lat_count)
@@ -151,28 +153,63 @@
         span = wide.at[pl.ds(half * pieces * LANES, pieces * LANES)]
         pltpu.make_async_copy(span, span, f_sem.at[half]).wait()
 
-    def table_source(i, target, start, stop):
+    def table_span(i, part):
+        return slice(part[0] - lows[i], part[1] - lows[i])
+
+    def lats_of(part):
+        return pl.ds(depth * portion, portion) if part[2] in shared else pl.ds(0, lat_rows)
+
+    def table_source(i, target, part):
         row = pl.multiple_of(block_of(i, target, lat_count) * SUB, SUB)
-        return g_ref.at[:, pl.ds(row, SUB), start:stop]
+        return g_ref.at[lats_of(part), pl.ds(row, SUB), part[0]:part[1]]
+
+    def table_target(i, part):
+        return t_refs[i].at[me, lats_of(part), :, table_span(i, part)]
 
     def table_send(i, part):
-        start, stop, sem = part
         for offset in range(1, lat_count):
             target = lat_peer(offset)
             pltpu.make_async_remote_copy(
-                src_ref=table_source(i, target, start, stop),
-                dst_ref=t_refs[i].at[me, :, :, start - lows[i]:stop - lows[i]],
-                send_sem=t_send.at[sem],
-                recv_sem=t_recv.at[sem],
+                src_ref=table_source(i, target, part),
+                dst_ref=table_target(i, part),
+                send_sem=t_send.at[part[2]],
+                recv_sem=t_recv.at[part[2]],
                 device_id={"lat": target},
                 device_id_type=pl.DeviceIdType.MESH,
             ).start()
 
-    def own_table(i):
-        return pltpu.make_async_copy(table_source(i, me, lows[i], totals), t_refs[i].at[me], own_sem.at[i])
+    def own_table(i, part):
+        return pltpu.make_async_copy(table_source(i, me, part), table_target(i, part), own_sem.at[part[2]])
+
+    def table_remote(i, part):
+        count = portion if part[2] in shared else lat_rows
+        return t_refs[i].at[pl.ds(0, lat_count - 1), pl.ds(0, count), :, table_span(i, part)]
+
+    def table_passed(i, part):
+        return t_refs[i].at[:, pl.ds(0, (lev_count - 1) * portion), :, table_span(i, part)]
+
+    def table_arrive(i, part):
+        own_table(i, part).wait()
+        settle(table_remote(i, part), t_recv.at[part[2]])
+
+    def table_pass(i, part):
+        table_arrive(i, part)
+        block = t_refs[i].at[:, lats_of(part), :, table_span(i, part)]
+        for offset in range(1, lev_count):
+            pltpu.make_async_remote_copy(
+                src_ref=block,
+                dst_ref=block,
+                send_sem=w_send.at[part[2]],
+                recv_sem=w_recv.at[part[2]],
+                device_id={"lev": lev_peer(offset)},
+                device_id_type=pl.DeviceIdType.MESH,
+            ).start()
+
+    def shared_parts():
+        return [(i, part) for i in range(blocks) for part in columns[i] if part[2] in shared]
 
     def own_spectra(i):
-        return pltpu.make_async_copy(sent.at[me, i], got.at[i, me], own_sem.at[blocks + i])
+        return pltpu.make_async_copy(sent.at[me, i], got.at[i, me], own_sem.at[blocks + 1 + i])
 
     def spectra_send(i, e):
         for offset in range(1, lat_count):
@@ -220,8 +257,11 @@
         )
     pl.semaphore_wait(barrier, lat_count + lev_count - 2)
     table_send(0, columns[0][0])
+    for i, part in shared_parts():
+        table_send(i, part)
     for i in range(blocks):
-        own_table(i).start()
+        for part in columns[i]:
+            own_table(i, part).start()
 
     rows_view = wide.reshape(wide.shape[0] * SUB, LANES)
     span = SUB * halves
@@ -288,16 +328,21 @@
 
         lax.fori_loop(0, lat_count, emit, 0)
         spectra_send(0, e)
+
+        @pl.when(e == steps // 2 - 1)
+        def _():
+            for i, part in shared_parts():
+                table_pass(i, part)
+
         return carry
 
     lax.fori_loop(0, steps, spectra_step, 0)
     for i in range(blocks):
         own_spectra(i).start()
-    for part in columns[0][1:]:
-        table_send(0, part)
     for i in range(1, blocks):
         for part in columns[i]:
-            table_send(i, part)
+            if part[2] not in shared:
+                table_send(i, part)
 
         def rest(e, carry):
             spectra_send(i, e)
@@ -320,7 +365,6 @@
     table_base = pairs * totals * SUB
 
     def legendre_sum(i):
-        own_table(i).wait()
         for n, part in enumerate(columns[i]):
             legendre_part(i, part, n == 0)
 
@@ -328,7 +372,10 @@
         left, right, sem = part
         width = right - left
         low = left - lows[i]
-        settle(t_refs[i].at[pl.ds(0, lat_count - 1), :, :, low:low + width], t_recv.at[sem])
+        if sem in shared:
+            settle(table_passed(i, part), w_recv.at[sem])
+        else:
+            table_arrive(i, part)
 
         def spread(source, carry):
             for w in range(width // LANES):
@@ -515,9 +562,10 @@
     settle(slots_out.at[pl.ds(0, lat_count - 1)], d_send)
     settle(sent.at[pl.ds(0, lat_count - 1)], s_send)
     for i in range(blocks):
-        for left, right, sem in columns[i]:
-            part = t_refs[i].at[pl.ds(0, lat_count - 1), :, :, left - lows[i]:right - lows[i]]
-            settle(part, t_send.at[sem])
+        for part in columns[i]:
+            settle(table_remote(i, part), t_send.at[part[2]])
+            if part[2] in shared:
+                settle(table_passed(i, part), w_send.at[part[2]])
 
         def drain(t, carry):
             for_waves(i, t, lambda copy: copy.wait_send())
@@ -569,7 +617,7 @@
             pltpu.VMEM((lat_count, share, lev_rows, levels), jnp.bfloat16),
             pltpu.VMEM((lat_count, share, lev_rows, levels), jnp.bfloat16),
             pltpu.SemaphoreType.DMA((2,)),
-            pltpu.SemaphoreType.DMA((2 * blocks,)),
+            pltpu.SemaphoreType.DMA((2 * blocks + 1,)),
             pltpu.SemaphoreType.DMA((blocks + 1,)),
             pltpu.SemaphoreType.DMA((blocks + 1,)),
             pltpu.SemaphoreType.DMA,
@@ -582,6 +630,8 @@
             pltpu.SemaphoreType.DMA,
             pltpu.SemaphoreType.DMA,
             pltpu.SemaphoreType.DMA,
+            pltpu.SemaphoreType.DMA((blocks + 1,)),
+            pltpu.SemaphoreType.DMA((blocks + 1,)),
         ],
         compiler_params=pltpu.CompilerParams(
             vmem_limit_bytes=VMEM_LIMIT, collective_id=0, has_side_effects=True
@@ -595,6 +645,7 @@
     modes = legendre.shape[1]
     fits = (
         lat_rows % 16 == 0
+        and lat_rows % lev_count == 0
         and members * lev_rows % LANES == 0
         and lev_rows * lev_count == LANES
         and lat_count == SUB

time: 231 us -> 237 us (1.026)
  Pallas kernels: 229 us -> 234 us
    pallas_call x1, Pallas kernels: 229 us -> 234 us  [on_device(): pl.pallas_call(functools.partial(main_kernel, size), out_shape=jax.ShapeD...]
where the time goes in v7:
time: 237 us; the launch traced here: 236 us
  Pallas kernels  234 us (99%)
    pallas_call x1, Pallas kernels, on_device(): pl.pallas_call(functools.partial(main_kernel, size), out_shape=jax.ShapeD...  234 us

profile of v7, /device:TPU:1, one launch (start us, length us, event | category | flops | bytes accessed | tf_op | source)
XLA Modules:
  0.0 236.4 jit_solution(3477601636144144535)
XLA Ops:
  0.0 234.1 %shard_map.64 = f32[64,32,128]{2,1,0:T(8,128)} custom-call(s32[8]{0:T(128)} %refs_0_.1, f32[384,4,8,1024]{3,2,1,0:T(8,128)} %bitcast.1, bf16[32,256,256]{2,1,0:T(8,128)(2,1)} %refs_2_.1, bf16[2,256,512]{2,1,0:T(8,128)(2,1)} %constant.6.clone.refs_3_, bf16[2,128,256]{2,1,0:T(8,128)(2,1)} %constant.7.clone.refs_4_, bf16[2,128,256]{2,1,0:T(8,128)(2,1)} %constant.8.clone.refs_5_), custom_call_target="tpu_custom_call" | custom-call | flops 40000000000 | bytes 80000000 | tf_op jit(solution)/shard_map/pallas_call | solution.py:599
  234.1 2.3 copy.8
